TPU v7x, 32 devices: a whole 2x2x4 slice. The times are simulated.
32 devices in a mesh: irrep: 4 (over z), occ: 4 (over y, core), vir: 2 (over x).
Axes of the slice: x: 2, y: 2, z: 4, core: 2. Of those that a mesh axis runs over, the one named last changes fastest.
Arguments:
- amplitudes: bfloat16 [8, 320, 12288], P('irrep', None, ('occ', 'vir')), may hold values from -6 to 6
- ladder_ints: bfloat16 [8, 12288, 12288], P('irrep', ('occ', 'vir')), may hold values from -0.078125 to 0.078125
- hole_ints: bfloat16 [8, 320, 320], P('irrep'), may hold values from -0.3125 to 0.3125
- occ_energy: float32 [8, 320], P('irrep'), may hold values from -3 to -0.5
- vir_energy: float32 [8, 12288], P('irrep', ('occ', 'vir')), may hold values from 0.5 to 3
- occ_pairs: int32 [8], replicated, may hold values from 160 to 320, as said below
- vir_pairs: int32 [8], replicated, may hold values from 6144 to 12288, as said below
Outputs:
- updated: bfloat16 [8, 320, 12288], P('irrep', None, ('occ', 'vir'))
- residual_norm: float32 [8], P('irrep')
Inputs may be any that keep to these rules, and one draw needn't show every extreme that they name: `occ_pairs`: some block has exactly 320 live occupied pairs in every draw. `vir_pairs`: some block has exactly 12288 live virtual pairs in every draw.
All inputs are finite; a program needn't handle non-finite values.
Results may differ from a plain program's by a relative error of at most 0.001.
Values may be sent and summed in bfloat16 or wider, within the bound.
No kernel may reach another device: no remote copies, remote signals or barrier semaphores. Data moves between devices by JAX's collectives and lax.ppermute only.
A program may use at most 192 MiB of HBM per device.

v0:
```python
import jax
import jax.numpy as jnp
from jax import lax
from jax.sharding import PartitionSpec as P

LEVEL_SHIFT = 0.5
EPSILON = 1e-06


def table_lookup(table, block_ids):
    entries = table.shape[0]
    match = jnp.arange(entries, dtype=jnp.int32)[None, :] == block_ids[:, None]
    return jnp.sum(jnp.where(match, table[None, :], 0), axis=1)


def body(amplitudes, ladder_ints, hole_ints, occ_energy, vir_energy, occ_pairs, vir_pairs):
    block_count, pair_rows, cols_here = amplitudes.shape
    vir_devices = lax.axis_size("vir")
    block_ids = lax.axis_index("irrep") * block_count + jnp.arange(block_count, dtype=jnp.int32)
    slot_index = lax.axis_index("occ") * vir_devices + lax.axis_index("vir")
    column_start = slot_index * cols_here
    occ_here = table_lookup(occ_pairs, block_ids)
    vir_here = table_lookup(vir_pairs, block_ids)
    row_index = jnp.arange(pair_rows, dtype=jnp.int32)
    col_index = column_start + jnp.arange(cols_here, dtype=jnp.int32)
    keep_mask = (row_index[None, :, None] < occ_here[:, None, None]) & (
        col_index[None, None, :] < vir_here[:, None, None]
    )
    masked = jnp.where(keep_mask, amplitudes, jnp.zeros((), amplitudes.dtype))
    product = jnp.einsum("hkc,hpk->chp", ladder_ints, masked, preferred_element_type=jnp.float32)
    summed = lax.psum_scatter(
        product.reshape(lax.axis_size(("occ", "vir")) * cols_here, block_count * pair_rows),
        ("occ", "vir"),
        scatter_dimension=0,
        tiled=True,
    )
    ladder_term = summed.reshape(cols_here, block_count, pair_rows).transpose(1, 2, 0)
    hole_term = jnp.einsum("hpr,hrq->hpq", hole_ints, masked, preferred_element_type=jnp.float32)
    wide = masked.astype(jnp.float32)
    denominator = vir_energy[:, None, :] - occ_energy[:, :, None]
    residual = jnp.where(
        keep_mask, ladder_term + hole_term + denominator * wide, jnp.zeros((), jnp.float32)
    )
    updated = (wide - residual / (denominator + LEVEL_SHIFT)).astype(jnp.bfloat16)
    squares = jnp.sum(residual * residual, axis=(1, 2))
    summed_squares = lax.psum(squares, ("occ", "vir"))
    pair_count = (occ_here * vir_here).astype(jnp.float32)
    residual_norm = jnp.sqrt(summed_squares / pair_count + EPSILON)
    return (updated, residual_norm)


def solution(mesh):
    in_specs = (
        P("irrep", None, ("occ", "vir")),
        P("irrep", ("occ", "vir"), None),
        P("irrep", None, None),
        P("irrep", None),
        P("irrep", ("occ", "vir")),
        P(),
        P(),
    )
    out_specs = (P("irrep", None, ("occ", "vir")), P("irrep"))
    return jax.shard_map(body, mesh=mesh, in_specs=in_specs, out_specs=out_specs, check_vma=False)
```

profile of v0, /device:TPU:0, one launch (start us, length us, event | category | flops | bytes accessed | tf_op | source)
XLA Modules:
  0.0 264.5 jit_solution(5050272577106343690)
XLA Ops:
  7.2 0.0 copy-start
  7.2 0.0 reduce-scatter.2.cloned.1.call-start
  7.2 0.9 select_reduce_fusion.1
  8.2 0.1 iota_compare_fusion
  8.2 0.1 broadcast_compare_fusion
  8.3 41.2 %fusion.3 = f32[2,320,12288]{2,1,0:T(8,128)} fusion(bf16[2,1536,12288]{2,1,0:T(8,128)(2,1)} %param.8, bf16[2,320,1536]{2,1,0:T(8,128)(2,1)} %param.7, pred[2,1536]{1,0:T(4,128)(4,1)S(1)} %broadcast_compare_fusion, pred[2,320]{1,0:T(4,128)(4,1)S(1)} %iota_compare_fusion), kind=kOutput, calls=%fused_computation.10 | convolution fusion | flops 24161157120 | bytes 108924544 | tf_op jit(solution)/shard_map/hkc,hpk->chp/dot_general | solution.py:30
  49.6 0.0 copy-start.1
  49.6 0.0 copy-start.2
  49.6 0.0 copy-start.3
  49.6 0.0 reduce-scatter.2.cloned.1.call-update
  49.6 188.7 %reduce-scatter.2.cloned.1.call-done = f32[1536,640]{0,1:T(8,128)} async-done(((f32[12288,640]{0,1:T(8,128)}), f32[1536,640]{0,1:T(8,128)}) %reduce-scatter.2.cloned.1.call-update) | async-done | bytes 3932176 | tf_op jit(solution)/shard_map/reduce_scatter | solution.py:31
  238.3 0.0 copy-done
  238.3 0.0 copy-done.1
  238.3 0.0 copy-done.2
  238.3 0.0 copy-done.3
  238.3 5.6 %multiply_reduce_fusion = (f32[2]{0:T(128)S(1)}, bf16[2,320,1536]{2,1,0:T(8,128)(2,1)}) fusion(f32[2,320]{1,0:T(2,128)S(1)} %copy-done.3, f32[2,1536]{1,0:T(2,128)S(1)} %copy-done.2, bf16[2,320,1536]{2,1,0:T(8,128)(2,1)S(1)} %copy-done.1, pred[2,1536]{1,0:T(4,128)(4,1)S(1)} %broadcast_compare_fusion, pred[2,320]{1,0:T(4,128)(4,1)S(1)} %iota_compare_fusion, ...), kind=kOutput, calls=%fused_computation.9 | convolution fusion | flops 644874240 | bytes 8292488 | tf_op jit(solution)/shard_map/hpr,hrq->hpq/dot_general | solution.py:38
  243.8 13.3 %psum.7 = f32[2]{0:T(128)S(1)} all-reduce(f32[2]{0:T(128)S(1)} %get-tuple-element.4), channel_id=1, replica_groups=mesh['irrep'=4,'occ'=4,'vir'=2] {'occ','vir'}, use_global_device_ids=true, to_apply=%region_4.5 | all-reduce | flops 2 | bytes 16 | tf_op jit(solution)/shard_map/psum | solution.py:46
  257.2 0.5 add_sqrt_fusion
  (2 shorter events, 0.0 us)
Async XLA Ops:
  7.2 231.1 %copy-start = (bf16[2,320,320]{2,1,0:T(8,128)(2,1)S(1)}, bf16[2,320,320]{2,1,0:T(8,128)(2,1)}, u32[]{:S(2)}) copy-start(bf16[2,320,320]{2,1,0:T(8,128)(2,1)} %param.9) | copy-start | bytes 1228804
  7.2 231.1 %reduce-scatter.2.cloned.1.call-start = ((), (), s32[]{:S(2)}) async-start(), calls=%async_computation.1 | async-start | bytes 35389440 | tf_op jit(solution)/shard_map/reduce_scatter | solution.py:31
  49.6 188.7 %copy-start.1 = (bf16[2,320,1536]{2,1,0:T(8,128)(2,1)S(1)}, bf16[2,320,1536]{2,1,0:T(8,128)(2,1)}, u32[]{:S(2)}) copy-start(bf16[2,320,1536]{2,1,0:T(8,128)(2,1)} %param.7) | copy-start | bytes 5898244
  49.6 188.7 %copy-start.2 = (f32[2,1536]{1,0:T(2,128)S(1)}, f32[2,1536]{1,0:T(2,128)}, u32[]{:S(2)}) copy-start(f32[2,1536]{1,0:T(2,128)} %param.11) | copy-start | bytes 36868
  49.6 188.7 %copy-start.3 = (f32[2,320]{1,0:T(2,128)S(1)}, f32[2,320]{1,0:T(2,128)}, u32[]{:S(2)}) copy-start(f32[2,320]{1,0:T(2,128)} %param.10) | copy-start | bytes 7684
Sparse Core Ops, SparseCore 0:
  49.7 188.4 reduce-scatter.1
where the time goes:
time: 265 us
  waiting for transfers between devices  189 us (71%)
  matrix products  46.8 us (18%)
  between operations  14.1 us (5%)
  blocking collectives  13.3 us (5%)
    reduce_scatter x1, waiting for transfers between devices, body(): lax.psum_scatter(product.reshape(lax.axis_size(('occ', 'vir')) * cols_her...  189 us
    dot_general x1, matrix products, body(): jnp.einsum('hkc,hpk->chp', ladder_ints, masked, preferred_element_type=jn...  41.2 us
    psum x1, blocking collectives, body(): summed_squares = lax.psum(squares, ('occ', 'vir'))  13.3 us
    dot_general x1, matrix products, body(): jnp.einsum('hpr,hrq->hpq', hole_ints, masked, preferred_element_type=jnp....  5.58 us
  transfers between devices with their start and end apart: 1, of which 1 were waited for; matrix products, arithmetic and copies ran while one was open for 0% of the time, Pallas kernels for 0%

commit v1 on v0

v1 whole, which is shorter than its diff:
```python
import functools

import jax
import jax.numpy as jnp
from jax import lax
from jax.experimental import pallas as pl
from jax.experimental.pallas import tpu as pltpu
from jax.sharding import PartitionSpec as P


LEVEL_SHIFT = 0.5
EPSILON = 1e-06
GROUP = ("occ", "vir")
LANES = 128
CODE_ROWS = 8
CODE_STEPS = 256.0
TOP = 32766.0
VMEM_LIMIT = 6 * 1024 * 1024
IN_VMEM = pl.BlockSpec(memory_space=pltpu.VMEM)
IN_HBM = pl.BlockSpec(memory_space=pltpu.HBM)
IN_SMEM = pl.BlockSpec(memory_space=pltpu.SMEM)


def stage_bits(mesh):
    devices = mesh.devices.reshape(mesh.shape["irrep"], -1)[0]
    bits = list(range(len(devices).bit_length() - 1))

    def same_chip(bit):
        where = getattr(devices[0], "coords", None)
        return where is not None and where == getattr(devices[1 << bit], "coords", None)

    near = [b for b in bits if same_chip(b)]
    return near + [b for b in bits if b not in near]


def turn_plan(width, order):
    other = order[:1] + order[:0:-1]
    if width % (6 * LANES) == 0:
        unit = width // 6
        return [
            (unit, 0, [order]),
            (unit, unit, [other]),
            (unit, 2 * unit, [order, other]),
            (unit, 4 * unit, [order, other]),
        ]
    for turns in (4, 3, 2):
        if width % (turns * LANES) == 0:
            unit = width // turns
            return [(unit, n * unit, [other if n % 2 else order]) for n in range(turns)]
    return [(width, 0, [order])]


def patterns(bits):
    found = [0]
    for b in bits:
        found = found + [m | (1 << b) for m in found]
    return found


def packet_shape(count, rows, width):
    tiles = count * (width // LANES)
    return (tiles * (rows // 2) + pl.cdiv(tiles, CODE_ROWS) * CODE_ROWS, LANES)


def row_of(table, n):
    here = lax.broadcasted_iota(jnp.int32, table.shape, 0) == n
    return jnp.sum(jnp.where(here, table, jnp.zeros_like(table)), axis=0, keepdims=True)


def unpack_add(total, packet, count, piece, rows, width):
    half = rows // 2
    tiles = width // LANES
    base = count * tiles * half
    out = []
    for t in range(tiles):
        n = piece * tiles + t
        codes = packet[pl.ds(pl.multiple_of(base + n // CODE_ROWS * CODE_ROWS, CODE_ROWS), CODE_ROWS), :]
        scales = jnp.exp2(codes.astype(jnp.float32) * (1.0 / CODE_STEPS)) * (1.0 / TOP)
        scale = row_of(scales, n % CODE_ROWS)
        words = packet[pl.ds(pl.multiple_of(n * half, CODE_ROWS), half), :]
        high = lax.shift_right_arithmetic(words, 16).astype(jnp.float32) * scale
        low = lax.shift_right_arithmetic(lax.shift_left(words, 16), 16).astype(jnp.float32) * scale
        a, b = total[t]
        out.append((a + high, b + low))
    return out


def pack_into(packet, total, count, piece, rows, width):
    half = rows // 2
    tiles = width // LANES
    base = count * tiles * half
    for t in range(tiles):
        n = piece * tiles + t
        a, b = total[t]
        peak = jnp.max(jnp.maximum(jnp.abs(a), jnp.abs(b)), axis=0, keepdims=True)
        level = jnp.ceil(jnp.log2(jnp.maximum(peak, 1e-30)) * CODE_STEPS) + 1.0
        factor = jnp.exp2(level * (-1.0 / CODE_STEPS)) * TOP
        high = jnp.round(a * factor).astype(jnp.int32)
        low = jnp.round(b * factor).astype(jnp.int32)
        packet[pl.ds(pl.multiple_of(n * half, CODE_ROWS), half), :] = lax.shift_left(high, 16) | (low & 0xFFFF)
        place = pl.ds(pl.multiple_of(base + n // CODE_ROWS * CODE_ROWS, CODE_ROWS), CODE_ROWS)
        here = lax.broadcasted_iota(jnp.int32, (CODE_ROWS, LANES), 0) == n % CODE_ROWS
        packet[place, :] = jnp.where(here, level.astype(jnp.int32), packet[place, :])


def lane_tiles(acc, rows, width):
    half = rows // 2
    return [
        (acc[:half, t * LANES : (t + 1) * LANES], acc[half:, t * LANES : (t + 1) * LANES])
        for t in range(width // LANES)
    ]


def my_slot():
    return lax.axis_index("occ") * lax.axis_size("vir") + lax.axis_index("vir")


def fetch(source, target, sems, block, spots, depth, width, n):
    mask, place = spots[n]
    first = (my_slot() ^ mask) * depth + place
    return pltpu.make_async_copy(
        source.at[block, :, pl.ds(pl.multiple_of(first, width), width)],
        target.at[block, n],
        sems.at[block, n],
    )


def fetch_all(source, target, sems, blocks, spots, depth, width, verb):
    for h in range(blocks):
        for n in range(len(spots)):
            getattr(fetch(source, target, sems, h, spots, depth, width, n), verb)()


def open_kernel(spots, width, source, pieces, sems):
    blocks, depth, _ = source.shape
    fetch_all(source, pieces, sems, blocks, spots, depth, width, "start")
    fetch_all(source, pieces, sems, blocks, spots, depth, width, "wait")


def open_call(ladder_ints, turn):
    block_count, depth, _ = ladder_ints.shape
    width, spots = turn
    return pl.pallas_call(
        functools.partial(open_kernel, spots, width),
        in_specs=[IN_HBM],
        out_specs=IN_VMEM,
        scratch_shapes=[pltpu.SemaphoreType.DMA((block_count, len(spots)))],
        out_shape=pltpu.VMEM((block_count, len(spots), depth, width), ladder_ints.dtype),
        compiler_params=pltpu.CompilerParams(vmem_limit_bytes=VMEM_LIMIT),
        name="open",
    )(ladder_ints)


def send_kernel(cfg, *refs):
    parts, count, first_col, recv_picks, own_picks, rows, width, _, next_width, next_spots, masking = cfg
    refs = list(refs)
    take = lambda n: [refs.pop(0) for _ in range(n)]
    own = own_picks is not None
    t_ref, source = take(2)
    occ_ref, vir_ref = take(2) if masking else (None, None)
    (pieces,) = take(1)
    recv_refs = [take(len(picks)) for picks in recv_picks]
    (hole_ref,) = take(1) if own else (None,)
    own_refs = [take(len(picks)) for picks in own_picks] if own else []
    out_refs = take(parts)
    (own_out,) = take(1) if own else (None,)
    (masked_ref,) = take(1) if masking else (None,)
    (next_pieces,) = take(1) if next_spots else (None,)
    blocks, _, depth = t_ref.shape

    if next_spots:
        (next_sems,) = take(1)
        fetch_all(source, next_pieces, next_sems, blocks, next_spots, depth, next_width, "start")
    half = rows // 2

    def step(block, carry):
        if masking:
            block_id = lax.axis_index("irrep") * blocks + block
            row_index = lax.broadcasted_iota(jnp.int32, (rows, depth), 0)
            col_index = lax.broadcasted_iota(jnp.int32, (rows, depth), 1)
            keep = (row_index < occ_ref[block_id]) & (col_index < vir_ref[block_id] - my_slot() * depth)
            masked_ref[block] = jnp.where(keep, t_ref[block].astype(jnp.float32), 0.0).astype(masked_ref.dtype)
        held_ref = masked_ref if masking else t_ref
        left = held_ref[block]

        def product(n):
            return jnp.dot(left, pieces[block, n], preferred_element_type=jnp.float32)

        for i in range(count):
            for c in range(parts):
                total = lane_tiles(product(i * parts + c), rows, width)
                for ref, (held, picks) in zip(recv_refs[c], recv_picks[c]):
                    total = unpack_add(total, ref, blocks * held, block * held + picks[i], rows, width)
                pack_into(out_refs[c], total, blocks * count, block * count + i, rows, width)
        if own:
            for c in range(parts):
                first = first_col + c * width
                acc = product(count * parts + c) + jnp.dot(
                    hole_ref[block], held_ref[block, :, first : first + width], preferred_element_type=jnp.float32
                )
                total = lane_tiles(acc, rows, width)
                for ref, (held, picks) in zip(own_refs[c], own_picks[c]):
                    total = unpack_add(total, ref, blocks * held, block * held + picks[0], rows, width)
                for t, (a, b) in enumerate(total):
                    cols = slice(c * width + t * LANES, c * width + (t + 1) * LANES)
                    own_out[block, :half, cols] = a
                    own_out[block, half:, cols] = b
        return carry

    lax.fori_loop(0, blocks, step, 0)
    if next_spots:
        fetch_all(source, next_pieces, next_sems, blocks, next_spots, depth, next_width, "wait")


def picks_of(recvs, wanted):
    return [(len(held), [held.index(m) for m in wanted]) for _, held in recvs]


def spots_of(width, first_col, masks, own):
    parts = len(masks)
    spots = [(masks[c][i], first_col + c * width) for i in range(len(masks[0])) for c in range(parts)]
    return spots + ([(0, first_col + c * width) for c in range(parts)] if own else [])


def send_call(t, ladder_ints, live, width, first_col, masks, recvs, own, pieces, next_turn):
    block_count, rows, depth = t.shape
    parts, count = len(masks), len(masks[0])
    both = parts * width
    masking = live is not None
    spots = spots_of(width, first_col, masks, own is not None)
    next_width, next_spots = next_turn
    in_specs, operands = [IN_VMEM, IN_HBM], [t, ladder_ints]
    if masking:
        in_specs += [IN_SMEM, IN_SMEM]
        operands += live
    in_specs.append(IN_VMEM)
    operands.append(pieces)
    for c in range(parts):
        in_specs += [IN_VMEM] * len(recvs[c])
        operands += [array for array, _ in recvs[c]]
    packet = pltpu.VMEM(packet_shape(block_count * count, rows, width), jnp.int32)
    out_shape = [packet] * parts
    own_picks = None
    if own is not None:
        hole_ints, own_recvs = own
        own_picks = [picks_of(r, [0]) for r in own_recvs]
        in_specs.append(IN_VMEM)
        operands.append(hole_ints)
        for c in range(parts):
            in_specs += [IN_VMEM] * len(own_recvs[c])
            operands += [array for array, _ in own_recvs[c]]
        out_shape.append(pltpu.VMEM((block_count, rows, both), jnp.float32))
    scratch = []
    if masking:
        out_shape.append(pltpu.VMEM(t.shape, t.dtype))
    if next_spots:
        out_shape.append(pltpu.VMEM((block_count, len(next_spots), depth, next_width), ladder_ints.dtype))
        scratch.append(pltpu.SemaphoreType.DMA((block_count, len(next_spots))))
    steps = block_count * len(spots)
    cost = pl.CostEstimate(
        flops=2 * steps * rows * depth * width, bytes_accessed=steps * 2 * depth * width, transcendentals=0
    )
    recv_picks = [picks_of(r, m) for r, m in zip(recvs, masks)]
    cfg = (parts, count, first_col, recv_picks, own_picks, rows, width, spots, next_width, next_spots, masking)
    return pl.pallas_call(
        functools.partial(send_kernel, cfg),
        in_specs=in_specs,
        out_specs=[IN_VMEM] * len(out_shape),
        scratch_shapes=scratch,
        out_shape=out_shape,
        cost_estimate=cost,
        compiler_params=pltpu.CompilerParams(vmem_limit_bytes=VMEM_LIMIT),
    )(*operands)


def finish_kernel(cfg, *refs):
    parts, rows, width, start, first_turn, want_update, want_squares, with_alias = cfg
    refs = list(refs)
    take = lambda n: [refs.pop(0) for _ in range(n)]
    own_ref, t_ref, occ_ref, vir_ref, occ_live_ref, vir_live_ref = take(6)
    recv_refs = take(parts)
    take(with_alias)
    (out_ref,) = take(1) if want_update else (None,)
    (sum_ref,) = take(1) if want_squares else (None,)
    block = pl.program_id(0)
    blocks, _, depth = t_ref.shape
    half = rows // 2
    tiles = width // LANES
    if first_turn:
        (column_ref,) = take(1)
        for r in range(0, rows, CODE_ROWS * 5):
            size = min(CODE_ROWS * 5, rows - r)
            row_index = lax.broadcasted_iota(jnp.int32, (size, rows), 0) + r
            col_index = lax.broadcasted_iota(jnp.int32, (size, rows), 1)
            occ = occ_ref[0:1, :]
            for h in range(1, blocks):
                occ = jnp.where(block == h, occ_ref[h : h + 1, :], occ)
            column = jnp.sum(jnp.where(row_index == col_index, occ, 0.0), axis=1, keepdims=True)
            column_ref[block, r : r + size, :] = jnp.broadcast_to(column, (size, LANES))
    else:
        column_ref = occ_ref
    block_id = lax.axis_index("irrep") * blocks + block
    occ_live = occ_live_ref[block_id]
    vir_live = vir_live_ref[block_id] - my_slot() * depth - start
    squares = jnp.zeros((CODE_ROWS, LANES), jnp.float32)
    row_index = lax.broadcasted_iota(jnp.int32, (half, LANES), 0)
    lane_index = lax.broadcasted_iota(jnp.int32, (half, LANES), 1)
    spans = [slice(0, half), slice(half, rows)]
    for c in range(parts):
        firsts = [c * width + t * LANES for t in range(tiles)]
        total = [tuple(own_ref[block, span, first : first + LANES] for span in spans) for first in firsts]
        total = unpack_add(total, recv_refs[c], blocks, block, rows, width)
        for t, first in enumerate(firsts):
            cols = slice(first, first + LANES)
            here = slice(start + first, start + first + LANES)
            vir = vir_ref[0:1, here]
            for h in range(1, blocks):
                vir = jnp.where(block == h, vir_ref[h : h + 1, here], vir)
            for part, span in enumerate(spans):
                keep = (row_index + part * half < occ_live) & (lane_index + first < vir_live)
                wide = t_ref[block, span, here].astype(jnp.float32)
                denominator = vir - column_ref[block, span, :]
                residual = jnp.where(keep, total[t][part] + denominator * wide, 0.0)
                if want_update:
                    out_ref[span, cols] = (wide - residual / (denominator + LEVEL_SHIFT)).astype(jnp.bfloat16)
                if want_squares:
                    squares += jnp.sum((residual * residual).reshape(-1, CODE_ROWS, LANES), axis=0)
    if want_squares:
        pair_count = jnp.full(squares.shape, occ_live * vir_live_ref[block_id], jnp.int32)
        sum_ref[...] = squares / pair_count.astype(jnp.float32)


def finish_call(t_masked, own, occ, vir_energy, live, width, start, recvs, updated, want_update, want_squares):
    block_count, rows, depth = t_masked.shape
    parts = len(recvs)
    both = parts * width
    first_turn = occ.ndim == 2
    operands = [own, t_masked, occ, vir_energy, *live] + [array for array, _ in recvs]
    in_specs = [IN_VMEM] * 4 + [IN_SMEM] * 2 + [IN_VMEM] * parts
    aliases = {}
    with_alias = int(want_update and updated is not None)
    if with_alias:
        in_specs.append(IN_HBM)
        operands.append(updated)
        aliases = {len(operands) - 1: 0}
    out_specs, out_shape = [], []
    if want_update:
        out_specs.append(pl.BlockSpec((None, rows, both), lambda h: (h, 0, start // both)))
        out_shape.append(jax.ShapeDtypeStruct((block_count, rows, depth), jnp.bfloat16))
    if want_squares:
        out_specs.append(pl.BlockSpec((None, CODE_ROWS, LANES), lambda h: (h, 0, 0)))
        out_shape.append(jax.ShapeDtypeStruct((block_count, CODE_ROWS, LANES), jnp.float32))
    if first_turn:
        out_specs.append(IN_VMEM)
        out_shape.append(jax.ShapeDtypeStruct((block_count, rows, LANES), jnp.float32))
    cfg = (parts, rows, width, start, first_turn, want_update, want_squares, with_alias)
    return pl.pallas_call(
        functools.partial(finish_kernel, cfg),
        grid=(block_count,),
        in_specs=in_specs,
        out_specs=out_specs,
        out_shape=out_shape,
        input_output_aliases=aliases,
        cost_estimate=pl.CostEstimate(
            flops=60 * block_count * rows * both, bytes_accessed=10 * block_count * rows * both, transcendentals=0
        ),
        compiler_params=pltpu.CompilerParams(dimension_semantics=("arbitrary",), vmem_limit_bytes=VMEM_LIMIT),
    )(*operands)


def job_order(turns, stages):
    jobs, far = [], []
    singles = turns[:2] if len(turns) > 2 else turns[:1]
    jobs += [(n, 0, True) for n in singles] + [(n, 1, None) for n in singles]
    far += list(singles)
    for n in turns[len(singles) :]:
        jobs += [(n, 0, True), (far.pop(0), 0, False), (n, 1, None)]
        far.append(n)
    if stages == 3 and len(turns) > 2:
        jobs += [(n, 2, None) for n in singles] + [(n, 0, False) for n in far]
        return jobs + [(n, 2, None) for n in turns[len(singles) :]]
    jobs += [(n, 0, False) for n in far]
    return jobs + [(n, t, None) for t in range(2, stages) for n in turns]


def body(order, *arrays):
    return residual_step(order, *arrays)


def residual_step(order, amplitudes, ladder_ints, hole_ints, occ_energy, vir_energy, occ_pairs, vir_pairs):
    _, _, cols_here = amplitudes.shape
    devices = lax.axis_size(GROUP)
    live = [occ_pairs, vir_pairs]

    def swap(packet, mask):
        return lax.ppermute(packet, GROUP, [(d, d ^ mask) for d in range(devices)])

    stages = len(order)
    plan = turn_plan(cols_here, order)
    turns = list(range(len(plan)))
    held = [[[] for _ in orders] for _, _, orders in plan]

    def having(turn, masks):
        return [[p for p in had if m[0] in p[1]] for had, m in zip(held[turn], masks)]

    calls = []
    for turn, t, near in job_order(turns, stages):
        orders = plan[turn][2]
        wanted = [patterns(o[2:] if t == 0 else o[t + 1 :]) for o in orders]
        if near:
            wanted = [[m | (1 << o[1]) for m in w] for o, w in zip(orders, wanted)]
        calls.append((turn, t, wanted, [[m | (1 << o[t]) for m in w] for o, w in zip(orders, wanted)]))
    spots = [
        (plan[turn][0], spots_of(plan[turn][0], plan[turn][1], masks, t == stages - 1)) for turn, t, _, masks in calls
    ] + [(0, None)]
    t_here, owns = amplitudes, {}
    pieces = open_call(ladder_ints, spots[0])
    for n, (turn, t, wanted, masks) in enumerate(calls):
        width, start, orders = plan[turn]
        parts = len(orders)
        own = (hole_ints, having(turn, [[0]] * parts)) if t == stages - 1 else None
        outs = send_call(
            t_here, ladder_ints, None if n else live, width, start, masks, having(turn, masks), own, pieces,
            spots[n + 1],
        )
        if own is not None:
            owns[turn] = outs[parts]
        if n == 0:
            t_here = outs[parts]
        if spots[n + 1][1]:
            pieces = outs[-1]
        for c, o in enumerate(orders):
            packet = outs[c]
            if t == stages - 1 and turn == turns[-1] - 1:
                packet = lax.optimization_barrier((packet, held[turns[-1]][0][-1][0]))[0]
            held[turn][c].append((swap(packet, 1 << o[t]), wanted[c]))
    updated, sums, occ = None, [], occ_energy
    for turn in turns:
        width, start, _ = plan[turn]

        def finish(want_update, want_squares):
            return finish_call(
                t_here, owns[turn], occ, vir_energy, live, width, start, [h[-1] for h in held[turn]], updated,
                want_update, want_squares,
            )

        if turn == turns[-1] and turn:
            (squares,) = finish(False, True)
            (updated,) = finish(True, False)
        else:
            updated, squares, *rest = finish(True, True)
            occ = rest[0] if rest else occ
        sums.append(squares)
    squares = jnp.sum(functools.reduce(jnp.add, sums), axis=(1, 2))
    squares = squares + swap(squares, 1 << order[0])
    across = []
    for mask in patterns(order[1:])[1:]:
        across.append(swap(squares, mask))
    residual_norm = jnp.sqrt(functools.reduce(jnp.add, [squares] + across) + EPSILON)
    return (updated, residual_norm)


def solution(mesh):
    in_specs = (
        P("irrep", None, ("occ", "vir")),
        P("irrep", ("occ", "vir"), None),
        P("irrep", None, None),
        P("irrep", None),
        P("irrep", ("occ", "vir")),
        P(),
        P(),
    )
    out_specs = (P("irrep", None, ("occ", "vir")), P("irrep"))
    order = stage_bits(mesh)
    return jax.shard_map(
        functools.partial(body, order), mesh=mesh, in_specs=in_specs, out_specs=out_specs, check_vma=False
    )
```

time: 265 us -> 109 us (0.41)
  waiting for transfers between devices: 189 us -> 28.7 us
  Pallas kernels: 0 us -> 54.7 us
  matrix products: 46.8 us -> 0 us
  starting transfers between devices: 0.04 us -> 23.6 us
  blocking collectives: 13.3 us -> 0 us
  between operations: 14.1 us -> 0.91 us
    reduce_scatter x1 -> x0, waiting for transfers between devices: 189 us -> none  [body(): lax.psum_scatter(product.reshape(lax.axis_size(('occ', 'vir')) * cols_her...]
    pallas_call x0 -> x22, Pallas kernels: none -> 54.7 us  [the longest x16 43.4 us: send_call(): pl.pallas_call(functools.partial(send_kernel, cfg), in_specs=in_specs, ou...]
    dot_general x2 -> x0, matrix products: 46.8 us -> none  [the longest x1 41.2 us: body(): jnp.einsum('hkc,hpk->chp', ladder_ints, masked, preferred_element_type=jn...]
    ppermute x0 -> x28, waiting for transfers between devices: none -> 28.7 us  [swap(): return lax.ppermute(packet, GROUP, [(d, d ^ mask) for d in range(devices)])]
    ppermute x0 -> x28, starting transfers between devices: none -> 23.6 us  [swap(): return lax.ppermute(packet, GROUP, [(d, d ^ mask) for d in range(devices)])]
    psum x1 -> x0, blocking collectives: 13.3 us -> none  [body(): summed_squares = lax.psum(squares, ('occ', 'vir'))]
  transfers between devices with their start and end apart: 1 -> 28, of which waited for: 1 -> 12; matrix products, arithmetic and copies ran while one was open for 0% -> 0% of each run, Pallas kernels for 0% -> 34%
where the time goes in v1:
time: 109 us
  Pallas kernels  54.7 us (50%)
  waiting for transfers between devices  28.7 us (26%)
  starting transfers between devices  23.6 us (22%)
    pallas_call x16, Pallas kernels, send_call(): pl.pallas_call(functools.partial(send_kernel, cfg), in_specs=in_specs, ou...  43.4 us
    ppermute x28, waiting for transfers between devices, swap(): return lax.ppermute(packet, GROUP, [(d, d ^ mask) for d in range(devices)])  28.7 us
    ppermute x28, starting transfers between devices, swap(): return lax.ppermute(packet, GROUP, [(d, d ^ mask) for d in range(devices)])  23.6 us
    pallas_call x5, Pallas kernels, finish_call(): pl.pallas_call(functools.partial(finish_kernel, cfg), grid=(block_count,)...  9.22 us
  transfers between devices with their start and end apart: 28, of which 12 were waited for; matrix products, arithmetic and copies ran while one was open for 0% of the time, Pallas kernels for 34%

profile of v1, /device:TPU:0, one launch (start us, length us, event | category | flops | bytes accessed | tf_op | source)
XLA Modules:
  0.0 108.9 jit_solution(14077121282957927547)
XLA Ops:
  0.7 2.1 %open.1.refs_4_ = bf16[2,2,1536,256]{3,2,1,0:T(8,128)(2,1)S(1)} custom-call(bf16[2,1536,12288]{2,1,0:T(8,128)(2,1)} %refs_1_.31), custom_call_target="tpu_custom_call" | custom-call | tf_op jit(solution)/shard_map/open/pallas_call | solution.py:143
  3.2 2.5 %shard_map.86 = (s32[1288,128]{1,0:T(8,128)S(1)}, bf16[2,320,1536]{2,1,0:T(8,128)(2,1)S(1)}, bf16[2,2,1536,256]{3,2,1,0:T(8,128)(2,1)S(1)}) custom-call(bf16[2,320,1536]{2,1,0:T(8,128)(2,1)S(1)} %copy-done.1, bf16[2,1536,12288]{2,1,0:T(8,128)(2,1)} %refs_1_.31, s32[8]{0:T(128)S(1)} %copy-done.3, s32[8]{0:T(128)S(1)} %copy-done.5, ...), custom_call_target="tpu_custom_call" | custom-call | flops 1006632960 | bytes 3145728 | tf_op jit(solution)/shard_map/pallas_call | solution.py:265
  6.2 1.9 %shard_map.87 = (s32[1288,128]{1,0:T(8,128)S(1)}, bf16[2,2,1536,256]{3,2,1,0:T(8,128)(2,1)S(1)}) custom-call(bf16[2,320,1536]{2,1,0:T(8,128)(2,1)S(1)} %get-tuple-element.55.refs_0_.refs_1_, bf16[2,1536,12288]{2,1,0:T(8,128)(2,1)} %refs_1_.31, bf16[2,2,1536,256]{3,2,1,0:T(8,128)(2,1)S(1)} %get-tuple-element.56.refs_2_), custom_call_target="tpu_custom_call" | custom-call | flops 1006632960 | bytes 3145728 | tf_op jit(solution)/shard_map/pallas_call | solution.py:265
  8.2 1.9 %shard_map.88 = (s32[1288,128]{1,0:T(8,128)S(1)}, bf16[2,2,1536,256]{3,2,1,0:T(8,128)(2,1)S(1)}) custom-call(bf16[2,320,1536]{2,1,0:T(8,128)(2,1)S(1)} %get-tuple-element.55.refs_0_.refs_1_, bf16[2,1536,12288]{2,1,0:T(8,128)(2,1)} %refs_1_.31, bf16[2,2,1536,256]{3,2,1,0:T(8,128)(2,1)S(1)} %get-tuple-element.57.refs_2_, ...), custom_call_target="tpu_custom_call" | custom-call | flops 1006632960 | bytes 3145728 | tf_op jit(solution)/shard_map/pallas_call | solution.py:265
  10.3 2.9 %shard_map.89 = (s32[1288,128]{1,0:T(8,128)S(1)}, bf16[2,4,1536,256]{3,2,1,0:T(8,128)(2,1)S(1)}) custom-call(bf16[2,320,1536]{2,1,0:T(8,128)(2,1)S(1)} %get-tuple-element.55.refs_0_.refs_1_, bf16[2,1536,12288]{2,1,0:T(8,128)(2,1)} %refs_1_.31, bf16[2,2,1536,256]{3,2,1,0:T(8,128)(2,1)S(1)} %get-tuple-element.59.refs_2_, ...), custom_call_target="tpu_custom_call" | custom-call | flops 1006632960 | bytes 3145728 | tf_op jit(solution)/shard_map/pallas_call | solution.py:265
  13.3 2.7 %shard_map.90 = (s32[1288,128]{1,0:T(8,128)S(1)}, s32[1288,128]{1,0:T(8,128)S(1)}, bf16[2,2,1536,256]{3,2,1,0:T(8,128)(2,1)S(1)}) custom-call(bf16[2,320,1536]{2,1,0:T(8,128)(2,1)S(1)} %get-tuple-element.55.refs_0_.refs_1_, bf16[2,1536,12288]{2,1,0:T(8,128)(2,1)} %refs_1_.31, bf16[2,4,1536,256]{3,2,1,0:T(8,128)(2,1)S(1)} %get-tuple-element.61.refs_2_), custom_call_target="tpu_custom_call" | custom-call | flops 2013265920 | bytes 6291456 | tf_op jit(solution)/shard_map/pallas_call | solution.py:265
  16.5 2.9 %shard_map.91 = (s32[1288,128]{1,0:T(8,128)S(1)}, bf16[2,4,1536,256]{3,2,1,0:T(8,128)(2,1)S(1)}) custom-call(bf16[2,320,1536]{2,1,0:T(8,128)(2,1)S(1)} %get-tuple-element.55.refs_0_.refs_1_, bf16[2,1536,12288]{2,1,0:T(8,128)(2,1)} %refs_1_.31, bf16[2,2,1536,256]{3,2,1,0:T(8,128)(2,1)S(1)} %get-tuple-element.62.refs_2_), custom_call_target="tpu_custom_call" | custom-call | flops 1006632960 | bytes 3145728 | tf_op jit(solution)/shard_map/pallas_call | solution.py:265
  19.5 3.0 %shard_map.92 = (s32[1288,128]{1,0:T(8,128)S(1)}, s32[1288,128]{1,0:T(8,128)S(1)}, bf16[2,4,1536,256]{3,2,1,0:T(8,128)(2,1)S(1)}) custom-call(bf16[2,320,1536]{2,1,0:T(8,128)(2,1)S(1)} %get-tuple-element.55.refs_0_.refs_1_, bf16[2,1536,12288]{2,1,0:T(8,128)(2,1)} %refs_1_.31, bf16[2,4,1536,256]{3,2,1,0:T(8,128)(2,1)S(1)} %get-tuple-element.63.refs_2_, ...), custom_call_target="tpu_custom_call" | custom-call | flops 2013265920 | bytes 6291456 | tf_op jit(solution)/shard_map/pallas_call | solution.py:265
  22.5 2.7 %shard_map.93 = (s32[1288,128]{1,0:T(8,128)S(1)}, s32[1288,128]{1,0:T(8,128)S(1)}, bf16[2,2,1536,256]{3,2,1,0:T(8,128)(2,1)S(1)}) custom-call(bf16[2,320,1536]{2,1,0:T(8,128)(2,1)S(1)} %get-tuple-element.55.refs_0_.refs_1_, bf16[2,1536,12288]{2,1,0:T(8,128)(2,1)} %refs_1_.31, bf16[2,4,1536,256]{3,2,1,0:T(8,128)(2,1)S(1)} %get-tuple-element.66.refs_2_), custom_call_target="tpu_custom_call" | custom-call | flops 2013265920 | bytes 6291456 | tf_op jit(solution)/shard_map/pallas_call | solution.py:265
  25.8 2.8 %collective-permute-start.6 = (s32[1288,128]{1,0:T(8,128)S(1)}, s32[1288,128]{1,0:T(8,128)S(1)}, u32[]{:S(2)}, u32[]{:S(2)}) collective-permute-start(s32[1288,128]{1,0:T(8,128)S(1)} %get-tuple-element.72), channel_id=1, source_target_pairs={{0,1},{1,0},{2,3},{3,2},{4,5},{5,4},{6,7},{7,6},{8,9},{9,8},{10,11... | collective-permute-start | bytes 1978376 | tf_op jit(solution)/shard_map/ppermute | solution.py:396
  28.6 1.5 %collective-permute-start.8 = (s32[1288,128]{1,0:T(8,128)S(1)}, s32[1288,128]{1,0:T(8,128)S(1)}, u32[]{:S(2)}, u32[]{:S(2)}) collective-permute-start(s32[1288,128]{1,0:T(8,128)S(1)} %get-tuple-element.75), channel_id=1, source_target_pairs={{0,4},{1,5},{2,6},{3,7},{4,0},{5,1},{6,2},{7,3},{8,12},{9,13},{10,... | collective-permute-start | bytes 1978376 | tf_op jit(solution)/shard_map/ppermute | solution.py:396
  30.1 2.9 %shard_map.94 = (s32[1288,128]{1,0:T(8,128)S(1)}, bf16[2,4,1536,256]{3,2,1,0:T(8,128)(2,1)S(1)}) custom-call(bf16[2,320,1536]{2,1,0:T(8,128)(2,1)S(1)} %get-tuple-element.55.refs_0_.refs_1_, bf16[2,1536,12288]{2,1,0:T(8,128)(2,1)} %refs_1_.31, bf16[2,2,1536,256]{3,2,1,0:T(8,128)(2,1)S(1)} %get-tuple-element.67.refs_2_), custom_call_target="tpu_custom_call" | custom-call | flops 1006632960 | bytes 3145728 | tf_op jit(solution)/shard_map/pallas_call | solution.py:265
  33.9 2.8 %shard_map.95 = (s32[1288,128]{1,0:T(8,128)S(1)}, s32[1288,128]{1,0:T(8,128)S(1)}, bf16[2,2,1536,256]{3,2,1,0:T(8,128)(2,1)S(1)}) custom-call(bf16[2,320,1536]{2,1,0:T(8,128)(2,1)S(1)} %get-tuple-element.55.refs_0_.refs_1_, bf16[2,1536,12288]{2,1,0:T(8,128)(2,1)} %refs_1_.31, bf16[2,4,1536,256]{3,2,1,0:T(8,128)(2,1)S(1)} %get-tuple-element.68.refs_2_, ...), custom_call_target="tpu_custom_call" | custom-call | flops 2013265920 | bytes 6291456 | tf_op jit(solution)/shard_map/pallas_call | solution.py:265
  36.7 7.6 %collective-permute-done.6.refs_3_.refs_6_ = s32[1288,128]{1,0:T(8,128)S(1)} collective-permute-done((s32[1288,128]{1,0:T(8,128)S(1)}, s32[1288,128]{1,0:T(8,128)S(1)}, u32[]{:S(2)}, u32[]{:S(2)}) %collective-permute-start.6) | collective-permute-done | bytes 659488 | tf_op jit(solution)/shard_map/ppermute | solution.py:396
  44.3 2.1 %collective-permute-start.12 = (s32[1288,128]{1,0:T(8,128)S(1)}, s32[1288,128]{1,0:T(8,128)S(1)}, u32[]{:S(2)}, u32[]{:S(2)}) collective-permute-start(s32[1288,128]{1,0:T(8,128)S(1)} %get-tuple-element.82), channel_id=1, source_target_pairs={{0,4},{1,5},{2,6},{3,7},{4,0},{5,1},{6,2},{7,3},{8,12},{9,13},{10,... | collective-permute-start | bytes 1978376 | tf_op jit(solution)/shard_map/ppermute | solution.py:396
  46.3 1.9 %shard_map.96 = (s32[648,128]{1,0:T(8,128)S(1)}, f32[2,320,256]{2,1,0:T(8,128)S(1)}, bf16[2,2,1536,256]{3,2,1,0:T(8,128)(2,1)S(1)}) custom-call(bf16[2,320,1536]{2,1,0:T(8,128)(2,1)S(1)} %get-tuple-element.55.refs_0_.refs_1_, bf16[2,1536,12288]{2,1,0:T(8,128)(2,1)} %refs_1_.31, bf16[2,2,1536,256]{3,2,1,0:T(8,128)(2,1)S(1)} %get-tuple-element.71.refs_2_, ...), custom_call_target="tpu_custom_call" | custom-call | flops 1006632960 | bytes 3145728 | tf_op jit(solution)/shard_map/pallas_call | solution.py:265
  48.3 3.0 %shard_map.97 = (s32[648,128]{1,0:T(8,128)S(1)}, f32[2,320,256]{2,1,0:T(8,128)S(1)}, bf16[2,4,1536,256]{3,2,1,0:T(8,128)(2,1)S(1)}) custom-call(bf16[2,320,1536]{2,1,0:T(8,128)(2,1)S(1)} %get-tuple-element.55.refs_0_.refs_1_, bf16[2,1536,12288]{2,1,0:T(8,128)(2,1)} %refs_1_.31, bf16[2,2,1536,256]{3,2,1,0:T(8,128)(2,1)S(1)} %get-tuple-element.74.refs_2_, ...), custom_call_target="tpu_custom_call" | custom-call | flops 1006632960 | bytes 3145728 | tf_op jit(solution)/shard_map/pallas_call | solution.py:265
  51.3 3.0 %shard_map.98 = (s32[1288,128]{1,0:T(8,128)S(1)}, s32[1288,128]{1,0:T(8,128)S(1)}, bf16[2,4,1536,256]{3,2,1,0:T(8,128)(2,1)S(1)}) custom-call(bf16[2,320,1536]{2,1,0:T(8,128)(2,1)S(1)} %get-tuple-element.55.refs_0_.refs_1_, bf16[2,1536,12288]{2,1,0:T(8,128)(2,1)} %refs_1_.31, bf16[2,4,1536,256]{3,2,1,0:T(8,128)(2,1)S(1)} %get-tuple-element.77.refs_2_), custom_call_target="tpu_custom_call" | custom-call | flops 2013265920 | bytes 6291456 | tf_op jit(solution)/shard_map/pallas_call | solution.py:265
  56.3 2.9 %shard_map.99 = (s32[1288,128]{1,0:T(8,128)S(1)}, s32[1288,128]{1,0:T(8,128)S(1)}, bf16[2,4,1536,256]{3,2,1,0:T(8,128)(2,1)S(1)}) custom-call(bf16[2,320,1536]{2,1,0:T(8,128)(2,1)S(1)} %get-tuple-element.55.refs_0_.refs_1_, bf16[2,1536,12288]{2,1,0:T(8,128)(2,1)} %refs_1_.31, bf16[2,4,1536,256]{3,2,1,0:T(8,128)(2,1)S(1)} %get-tuple-element.78.refs_2_), custom_call_target="tpu_custom_call" | custom-call | flops 2013265920 | bytes 6291456 | tf_op jit(solution)/shard_map/pallas_call | solution.py:265
  62.1 3.2 %shard_map.100 = (s32[648,128]{1,0:T(8,128)S(1)}, s32[648,128]{1,0:T(8,128)S(1)}, f32[2,320,512]{2,1,0:T(8,128)S(1)}, bf16[2,4,1536,256]{3,2,1,0:T(8,128)(2,1)S(1)}) custom-call(bf16[2,320,1536]{2,1,0:T(8,128)(2,1)S(1)} %get-tuple-element.55.refs_0_.refs_1_, bf16[2,1536,12288]{2,1,0:T(8,128)(2,1)} %refs_1_.31, ...), custom_call_target="tpu_custom_call" | custom-call | flops 2013265920 | bytes 6291456 | tf_op jit(solution)/shard_map/pallas_call | solution.py:265
  65.3 6.7 %collective-permute-done.14.refs_3_.refs_8_ = s32[1288,128]{1,0:T(8,128)S(1)} collective-permute-done((s32[1288,128]{1,0:T(8,128)S(1)}, s32[1288,128]{1,0:T(8,128)S(1)}, u32[]{:S(2)}, u32[]{:S(2)}) %collective-permute-start.14) | collective-permute-done | bytes 659488 | tf_op jit(solution)/shard_map/ppermute | solution.py:396
  72.0 1.7 %collective-permute-start.23 = (s32[648,128]{1,0:T(8,128)S(1)}, s32[648,128]{1,0:T(8,128)S(1)}, u32[]{:S(2)}, u32[]{:S(2)}) collective-permute-start(s32[648,128]{1,0:T(8,128)S(1)} %get-tuple-element.101), channel_id=1, source_target_pairs={{0,1},{1,0},{2,3},{3,2},{4,5},{5,4},{6,7},{7,6},{8,9},{9,8},{10,11... | collective-permute-start | bytes 995336 | tf_op jit(solution)/shard_map/ppermute | solution.py:396
  73.7 4.0 %collective-permute-done.16.refs_5_.refs_10_ = s32[1288,128]{1,0:T(8,128)S(1)} collective-permute-done((s32[1288,128]{1,0:T(8,128)S(1)}, s32[1288,128]{1,0:T(8,128)S(1)}, u32[]{:S(2)}, u32[]{:S(2)}) %collective-permute-start.16) | collective-permute-done | bytes 659488 | tf_op jit(solution)/shard_map/ppermute | solution.py:396
  77.8 3.1 %shard_map.101 = (s32[648,128]{1,0:T(8,128)S(1)}, s32[648,128]{1,0:T(8,128)S(1)}, f32[2,320,512]{2,1,0:T(8,128)S(1)}) custom-call(bf16[2,320,1536]{2,1,0:T(8,128)(2,1)S(1)} %get-tuple-element.55.refs_0_.refs_1_, bf16[2,1536,12288]{2,1,0:T(8,128)(2,1)} %refs_1_.31, bf16[2,4,1536,256]{3,2,1,0:T(8,128)(2,1)S(1)} %get-tuple-element.84.refs_2_, ...), custom_call_target="tpu_custom_call" | custom-call | flops 2013265920 | bytes 6291456 | tf_op jit(solution)/shard_map/pallas_call | solution.py:265
  80.9 1.6 %collective-permute-start.19 = (s32[648,128]{1,0:T(8,128)S(1)}, s32[648,128]{1,0:T(8,128)S(1)}, u32[]{:S(2)}, u32[]{:S(2)}) collective-permute-start(s32[648,128]{1,0:T(8,128)S(1)} %get-tuple-element.93), channel_id=1, source_target_pairs={{0,4},{1,5},{2,6},{3,7},{4,0},{5,1},{6,2},{7,3},{8,12},{9,13},{10,... | collective-permute-start | bytes 995336 | tf_op jit(solution)/shard_map/ppermute | solution.py:396
  86.3 1.8 %shard_map.102 = (bf16[2,320,1536]{2,1,0:T(8,128)(2,1)}, f32[2,8,128]{2,1,0:T(8,128)S(1)}, f32[2,320,128]{2,1,0:T(8,128)S(1)}) custom-call(f32[2,320,256]{2,1,0:T(8,128)S(1)} %get-tuple-element.90.refs_0_, bf16[2,320,1536]{2,1,0:T(8,128)(2,1)S(1)} %get-tuple-element.55.refs_0_.refs_1_, f32[2,320]{1,0:T(2,128)S(1)} %copy-done.7, f32[2,1536]{1,0:T(2,128)S(1)} %copy-done.2, ...), custom_call_target="tpu_custom_call" | custom-call | flops 9830400 | bytes 1638400 | tf_op jit(solution)/shard_map/pallas_call | solution.py:357
  88.1 1.7 %shard_map.103 = (bf16[2,320,1536]{2,1,0:T(8,128)(2,1)}, f32[2,8,128]{2,1,0:T(8,128)S(1)}) custom-call(f32[2,320,256]{2,1,0:T(8,128)S(1)} %get-tuple-element.100.refs_0_, bf16[2,320,1536]{2,1,0:T(8,128)(2,1)S(1)} %get-tuple-element.55.refs_0_.refs_1_, f32[2,320,128]{2,1,0:T(8,128)S(1)} %get-tuple-element.92.refs_2_, ...), custom_call_target="tpu_custom_call", output_to_operand_aliasing={{0}: (7, {})} | custom-call | flops 9830400 | bytes 1638400 | tf_op jit(solution)/shard_map/pallas_call | solution.py:357
  89.8 2.1 %collective-permute-done.19.refs_6_ = s32[648,128]{1,0:T(8,128)S(1)} collective-permute-done((s32[648,128]{1,0:T(8,128)S(1)}, s32[648,128]{1,0:T(8,128)S(1)}, u32[]{:S(2)}, u32[]{:S(2)}) %collective-permute-start.19) | collective-permute-done | bytes 331808 | tf_op jit(solution)/shard_map/ppermute | solution.py:396
  93.8 4.0 %collective-permute-done.21.refs_6_ = s32[648,128]{1,0:T(8,128)S(1)} collective-permute-done((s32[648,128]{1,0:T(8,128)S(1)}, s32[648,128]{1,0:T(8,128)S(1)}, u32[]{:S(2)}, u32[]{:S(2)}) %collective-permute-start.21) | collective-permute-done | bytes 331808 | tf_op jit(solution)/shard_map/ppermute | solution.py:396
  97.9 2.2 %shard_map.104 = (bf16[2,320,1536]{2,1,0:T(8,128)(2,1)}, f32[2,8,128]{2,1,0:T(8,128)S(1)}) custom-call(f32[2,320,512]{2,1,0:T(8,128)S(1)} %get-tuple-element.95.refs_0_, bf16[2,320,1536]{2,1,0:T(8,128)(2,1)S(1)} %get-tuple-element.55.refs_0_.refs_1_, f32[2,320,128]{2,1,0:T(8,128)S(1)} %get-tuple-element.92.refs_2_, ...), custom_call_target="tpu_custom_call", output_to_operand_aliasing={{0}: (8, {})} | custom-call | flops 19660800 | bytes 3276800 | tf_op jit(solution)/shard_map/pallas_call | solution.py:357
  100.2 2.2 %shard_map.105 = bf16[2,320,1536]{2,1,0:T(8,128)(2,1)} custom-call(f32[2,320,512]{2,1,0:T(8,128)S(1)} %get-tuple-element.89.refs_0_, bf16[2,320,1536]{2,1,0:T(8,128)(2,1)S(1)} %get-tuple-element.55.refs_0_.refs_1_, f32[2,320,128]{2,1,0:T(8,128)S(1)} %get-tuple-element.92.refs_2_, f32[2,1536]{1,0:T(2,128)S(1)} %copy-done.2, ...), custom_call_target="tpu_custom_call", output_to_operand_aliasing={{}: (8, {})} | custom-call | flops 19660800 | bytes 3276800 | tf_op jit(solution)/shard_map/pallas_call | solution.py:357
  102.4 2.1 %collective-permute-start.27 = (f32[2]{0:T(128)S(1)}, f32[2]{0:T(128)S(1)}, u32[]{:S(2)}, u32[]{:S(2)}) collective-permute-start(f32[2]{0:T(128)S(1)} %add.27), channel_id=1, source_target_pairs={{0,5},{1,4},{2,7},{3,6},{4,1},{5,0},{6,3},{7,2},{8,13},{9,12},{10,... | collective-permute-start | bytes 32 | tf_op jit(solution)/shard_map/ppermute | solution.py:396
  (65 shorter events, 18.5 us)
Async XLA Ops:
  5.7 2.6 %collective-permute-start = (s32[1288,128]{1,0:T(8,128)S(1)}, s32[1288,128]{1,0:T(8,128)S(1)}, u32[]{:S(2)}, u32[]{:S(2)}) collective-permute-start(s32[1288,128]{1,0:T(8,128)S(1)} %get-tuple-element.58), channel_id=1, source_target_pairs={{0,2},{1,3},{2,0},{3,1},{4,6},{5,7},{6,4},{7,5},{8,10},{9,11},{10,... | collective-permute-start | bytes 1978376 | tf_op jit(solution)/shard_map/ppermute | solution.py:396
  8.1 2.2 %collective-permute-start.1 = (s32[1288,128]{1,0:T(8,128)S(1)}, s32[1288,128]{1,0:T(8,128)S(1)}, u32[]{:S(2)}, u32[]{:S(2)}) collective-permute-start(s32[1288,128]{1,0:T(8,128)S(1)} %get-tuple-element.60), channel_id=1, source_target_pairs={{0,2},{1,3},{2,0},{3,1},{4,6},{5,7},{6,4},{7,5},{8,10},{9,11},{10,... | collective-permute-start | bytes 1978376 | tf_op jit(solution)/shard_map/ppermute | solution.py:396
  16.0 3.5 %collective-permute-start.2 = (s32[1288,128]{1,0:T(8,128)S(1)}, s32[1288,128]{1,0:T(8,128)S(1)}, u32[]{:S(2)}, u32[]{:S(2)}) collective-permute-start(s32[1288,128]{1,0:T(8,128)S(1)} %get-tuple-element.64), channel_id=1, source_target_pairs={{0,2},{1,3},{2,0},{3,1},{4,6},{5,7},{6,4},{7,5},{8,10},{9,11},{10,... | collective-permute-start | bytes 1978376 | tf_op jit(solution)/shard_map/ppermute | solution.py:396
  16.4 3.1 %collective-permute-start.3 = (s32[1288,128]{1,0:T(8,128)S(1)}, s32[1288,128]{1,0:T(8,128)S(1)}, u32[]{:S(2)}, u32[]{:S(2)}) collective-permute-start(s32[1288,128]{1,0:T(8,128)S(1)} %get-tuple-element.65), channel_id=1, source_target_pairs={{0,2},{1,3},{2,0},{3,1},{4,6},{5,7},{6,4},{7,5},{8,10},{9,11},{10,... | collective-permute-start | bytes 1978376 | tf_op jit(solution)/shard_map/ppermute | solution.py:396
  25.2 7.9 %collective-permute-start.4 = (s32[1288,128]{1,0:T(8,128)S(1)}, s32[1288,128]{1,0:T(8,128)S(1)}, u32[]{:S(2)}, u32[]{:S(2)}) collective-permute-start(s32[1288,128]{1,0:T(8,128)S(1)} %get-tuple-element.69), channel_id=1, source_target_pairs={{0,2},{1,3},{2,0},{3,1},{4,6},{5,7},{6,4},{7,5},{8,10},{9,11},{10,... | collective-permute-start | bytes 1978376 | tf_op jit(solution)/shard_map/ppermute | solution.py:396
  25.6 7.8 %collective-permute-start.5 = (s32[1288,128]{1,0:T(8,128)S(1)}, s32[1288,128]{1,0:T(8,128)S(1)}, u32[]{:S(2)}, u32[]{:S(2)}) collective-permute-start(s32[1288,128]{1,0:T(8,128)S(1)} %get-tuple-element.70), channel_id=1, source_target_pairs={{0,2},{1,3},{2,0},{3,1},{4,6},{5,7},{6,4},{7,5},{8,10},{9,11},{10,... | collective-permute-start | bytes 1978376 | tf_op jit(solution)/shard_map/ppermute | solution.py:396
  25.8 18.5 %collective-permute-start.6 = (s32[1288,128]{1,0:T(8,128)S(1)}, s32[1288,128]{1,0:T(8,128)S(1)}, u32[]{:S(2)}, u32[]{:S(2)}) collective-permute-start(s32[1288,128]{1,0:T(8,128)S(1)} %get-tuple-element.72), channel_id=1, source_target_pairs={{0,1},{1,0},{2,3},{3,2},{4,5},{5,4},{6,7},{7,6},{8,9},{9,8},{10,11... | collective-permute-start | bytes 1978376 | tf_op jit(solution)/shard_map/ppermute | solution.py:396
  28.6 17.7 %collective-permute-start.7 = (s32[1288,128]{1,0:T(8,128)S(1)}, s32[1288,128]{1,0:T(8,128)S(1)}, u32[]{:S(2)}, u32[]{:S(2)}) collective-permute-start(s32[1288,128]{1,0:T(8,128)S(1)} %get-tuple-element.73), channel_id=1, source_target_pairs={{0,2},{1,3},{2,0},{3,1},{4,6},{5,7},{6,4},{7,5},{8,10},{9,11},{10,... | collective-permute-start | bytes 1978376 | tf_op jit(solution)/shard_map/ppermute | solution.py:396
  28.6 19.7 %collective-permute-start.8 = (s32[1288,128]{1,0:T(8,128)S(1)}, s32[1288,128]{1,0:T(8,128)S(1)}, u32[]{:S(2)}, u32[]{:S(2)}) collective-permute-start(s32[1288,128]{1,0:T(8,128)S(1)} %get-tuple-element.75), channel_id=1, source_target_pairs={{0,4},{1,5},{2,6},{3,7},{4,0},{5,1},{6,2},{7,3},{8,12},{9,13},{10,... | collective-permute-start | bytes 1978376 | tf_op jit(solution)/shard_map/ppermute | solution.py:396
  33.1 15.2 %collective-permute-start.9 = (s32[1288,128]{1,0:T(8,128)S(1)}, s32[1288,128]{1,0:T(8,128)S(1)}, u32[]{:S(2)}, u32[]{:S(2)}) collective-permute-start(s32[1288,128]{1,0:T(8,128)S(1)} %get-tuple-element.76), channel_id=1, source_target_pairs={{0,2},{1,3},{2,0},{3,1},{4,6},{5,7},{6,4},{7,5},{8,10},{9,11},{10,... | collective-permute-start | bytes 1978376 | tf_op jit(solution)/shard_map/ppermute | solution.py:396
  33.4 25.9 %collective-permute-start.10 = (s32[1288,128]{1,0:T(8,128)S(1)}, s32[1288,128]{1,0:T(8,128)S(1)}, u32[]{:S(2)}, u32[]{:S(2)}) collective-permute-start(s32[1288,128]{1,0:T(8,128)S(1)} %get-tuple-element.80), channel_id=1, source_target_pairs={{0,1},{1,0},{2,3},{3,2},{4,5},{5,4},{6,7},{7,6},{8,9},{9,8},{10,11... | collective-permute-start | bytes 1978376 | tf_op jit(solution)/shard_map/ppermute | solution.py:396
  33.9 12.4 %copy-start = (bf16[2,320,320]{2,1,0:T(8,128)(2,1)S(1)}, bf16[2,320,320]{2,1,0:T(8,128)(2,1)}, u32[]{:S(2)}) copy-start(bf16[2,320,320]{2,1,0:T(8,128)(2,1)} %refs_7_.3) | copy-start | bytes 1228804
  44.3 15.8 %collective-permute-start.12 = (s32[1288,128]{1,0:T(8,128)S(1)}, s32[1288,128]{1,0:T(8,128)S(1)}, u32[]{:S(2)}, u32[]{:S(2)}) collective-permute-start(s32[1288,128]{1,0:T(8,128)S(1)} %get-tuple-element.82), channel_id=1, source_target_pairs={{0,4},{1,5},{2,6},{3,7},{4,0},{5,1},{6,2},{7,3},{8,12},{9,13},{10,... | collective-permute-start | bytes 1978376 | tf_op jit(solution)/shard_map/ppermute | solution.py:396
  54.2 7.3 %collective-permute-start.11 = (s32[1288,128]{1,0:T(8,128)S(1)}, s32[1288,128]{1,0:T(8,128)S(1)}, u32[]{:S(2)}, u32[]{:S(2)}) collective-permute-start(s32[1288,128]{1,0:T(8,128)S(1)} %get-tuple-element.81), channel_id=1, source_target_pairs={{0,2},{1,3},{2,0},{3,1},{4,6},{5,7},{6,4},{7,5},{8,10},{9,11},{10,... | collective-permute-start | bytes 1978376 | tf_op jit(solution)/shard_map/ppermute | solution.py:396
  54.3 7.2 %collective-permute-start.13 = (s32[1288,128]{1,0:T(8,128)S(1)}, s32[1288,128]{1,0:T(8,128)S(1)}, u32[]{:S(2)}, u32[]{:S(2)}) collective-permute-start(s32[1288,128]{1,0:T(8,128)S(1)} %get-tuple-element.83), channel_id=1, source_target_pairs={{0,2},{1,3},{2,0},{3,1},{4,6},{5,7},{6,4},{7,5},{8,10},{9,11},{10,... | collective-permute-start | bytes 1978376 | tf_op jit(solution)/shard_map/ppermute | solution.py:396
  54.8 17.2 %collective-permute-start.14 = (s32[1288,128]{1,0:T(8,128)S(1)}, s32[1288,128]{1,0:T(8,128)S(1)}, u32[]{:S(2)}, u32[]{:S(2)}) collective-permute-start(s32[1288,128]{1,0:T(8,128)S(1)} %get-tuple-element.85), channel_id=1, source_target_pairs={{0,1},{1,0},{2,3},{3,2},{4,5},{5,4},{6,7},{7,6},{8,9},{9,8},{10,11... | collective-permute-start | bytes 1978376 | tf_op jit(solution)/shard_map/ppermute | solution.py:396
  59.2 14.5 %collective-permute-start.15 = (s32[1288,128]{1,0:T(8,128)S(1)}, s32[1288,128]{1,0:T(8,128)S(1)}, u32[]{:S(2)}, u32[]{:S(2)}) collective-permute-start(s32[1288,128]{1,0:T(8,128)S(1)} %get-tuple-element.86), channel_id=1, source_target_pairs={{0,2},{1,3},{2,0},{3,1},{4,6},{5,7},{6,4},{7,5},{8,10},{9,11},{10,... | collective-permute-start | bytes 1978376 | tf_op jit(solution)/shard_map/ppermute | solution.py:396
  60.0 17.7 %collective-permute-start.16 = (s32[1288,128]{1,0:T(8,128)S(1)}, s32[1288,128]{1,0:T(8,128)S(1)}, u32[]{:S(2)}, u32[]{:S(2)}) collective-permute-start(s32[1288,128]{1,0:T(8,128)S(1)} %get-tuple-element.87), channel_id=1, source_target_pairs={{0,4},{1,5},{2,6},{3,7},{4,0},{5,1},{6,2},{7,3},{8,12},{9,13},{10,... | collective-permute-start | bytes 1978376 | tf_op jit(solution)/shard_map/ppermute | solution.py:396
  61.5 16.2 %collective-permute-start.17 = (s32[1288,128]{1,0:T(8,128)S(1)}, s32[1288,128]{1,0:T(8,128)S(1)}, u32[]{:S(2)}, u32[]{:S(2)}) collective-permute-start(s32[1288,128]{1,0:T(8,128)S(1)} %get-tuple-element.88), channel_id=1, source_target_pairs={{0,2},{1,3},{2,0},{3,1},{4,6},{5,7},{6,4},{7,5},{8,10},{9,11},{10,... | collective-permute-start | bytes 1978376 | tf_op jit(solution)/shard_map/ppermute | solution.py:396
  61.5 23.3 %collective-permute-start.18 = (s32[648,128]{1,0:T(8,128)S(1)}, s32[648,128]{1,0:T(8,128)S(1)}, u32[]{:S(2)}, u32[]{:S(2)}) collective-permute-start(s32[648,128]{1,0:T(8,128)S(1)} %get-tuple-element.91), channel_id=1, source_target_pairs={{0,4},{1,5},{2,6},{3,7},{4,0},{5,1},{6,2},{7,3},{8,12},{9,13},{10,... | collective-permute-start | bytes 995336 | tf_op jit(solution)/shard_map/ppermute | solution.py:396
  72.0 16.1 %collective-permute-start.23 = (s32[648,128]{1,0:T(8,128)S(1)}, s32[648,128]{1,0:T(8,128)S(1)}, u32[]{:S(2)}, u32[]{:S(2)}) collective-permute-start(s32[648,128]{1,0:T(8,128)S(1)} %get-tuple-element.101), channel_id=1, source_target_pairs={{0,1},{1,0},{2,3},{3,2},{4,5},{5,4},{6,7},{7,6},{8,9},{9,8},{10,11... | collective-permute-start | bytes 995336 | tf_op jit(solution)/shard_map/ppermute | solution.py:396
  77.7 8.6 %copy-start.2 = (f32[2,1536]{1,0:T(2,128)S(1)}, f32[2,1536]{1,0:T(2,128)}, u32[]{:S(2)}) copy-start(f32[2,1536]{1,0:T(2,128)} %refs_3_.11) | copy-start | bytes 36868
  77.7 8.6 %copy-start.4 = (s32[8]{0:T(128)S(1)}, s32[8]{0:T(128)}, u32[]{:S(2)}) copy-start(s32[8]{0:T(128)} %refs_4_.9) | copy-start | bytes 100
  77.7 8.6 %copy-start.6 = (s32[8]{0:T(128)S(1)}, s32[8]{0:T(128)}, u32[]{:S(2)}) copy-start(s32[8]{0:T(128)} %refs_5_.13) | copy-start | bytes 100
  80.9 11.1 %collective-permute-start.19 = (s32[648,128]{1,0:T(8,128)S(1)}, s32[648,128]{1,0:T(8,128)S(1)}, u32[]{:S(2)}, u32[]{:S(2)}) collective-permute-start(s32[648,128]{1,0:T(8,128)S(1)} %get-tuple-element.93), channel_id=1, source_target_pairs={{0,4},{1,5},{2,6},{3,7},{4,0},{5,1},{6,2},{7,3},{8,12},{9,13},{10,... | collective-permute-start | bytes 995336 | tf_op jit(solution)/shard_map/ppermute | solution.py:396
  82.5 10.0 %collective-permute-start.20 = (s32[648,128]{1,0:T(8,128)S(1)}, s32[648,128]{1,0:T(8,128)S(1)}, u32[]{:S(2)}, u32[]{:S(2)}) collective-permute-start(s32[648,128]{1,0:T(8,128)S(1)} %get-tuple-element.94), channel_id=1, source_target_pairs={{0,1},{1,0},{2,3},{3,2},{4,5},{5,4},{6,7},{7,6},{8,9},{9,8},{10,11... | collective-permute-start | bytes 995336 | tf_op jit(solution)/shard_map/ppermute | solution.py:396
  83.9 13.9 %collective-permute-start.21 = (s32[648,128]{1,0:T(8,128)S(1)}, s32[648,128]{1,0:T(8,128)S(1)}, u32[]{:S(2)}, u32[]{:S(2)}) collective-permute-start(s32[648,128]{1,0:T(8,128)S(1)} %get-tuple-element.97), channel_id=1, source_target_pairs={{0,4},{1,5},{2,6},{3,7},{4,0},{5,1},{6,2},{7,3},{8,12},{9,13},{10,... | collective-permute-start | bytes 995336 | tf_op jit(solution)/shard_map/ppermute | solution.py:396
  84.8 13.0 %collective-permute-start.22 = (s32[648,128]{1,0:T(8,128)S(1)}, s32[648,128]{1,0:T(8,128)S(1)}, u32[]{:S(2)}, u32[]{:S(2)}) collective-permute-start(s32[648,128]{1,0:T(8,128)S(1)} %get-tuple-element.99), channel_id=1, source_target_pairs={{0,1},{1,0},{2,3},{3,2},{4,5},{5,4},{6,7},{7,6},{8,9},{9,8},{10,11... | collective-permute-start | bytes 995336 | tf_op jit(solution)/shard_map/ppermute | solution.py:396
  100.2 2.2 %collective-permute-start.24 = (f32[2]{0:T(128)S(1)}, f32[2]{0:T(128)S(1)}, u32[]{:S(2)}, u32[]{:S(2)}) collective-permute-start(f32[2]{0:T(128)S(1)} %add_reduce_fusion), channel_id=1, source_target_pairs={{0,2},{1,3},{2,0},{3,1},{4,6},{5,7},{6,4},{7,5},{8,10},{9,11},{10,... | collective-permute-start | bytes 32 | tf_op jit(solution)/shard_map/ppermute | solution.py:396
  102.4 4.5 %collective-permute-start.27 = (f32[2]{0:T(128)S(1)}, f32[2]{0:T(128)S(1)}, u32[]{:S(2)}, u32[]{:S(2)}) collective-permute-start(f32[2]{0:T(128)S(1)} %add.27), channel_id=1, source_target_pairs={{0,5},{1,4},{2,7},{3,6},{4,1},{5,0},{6,3},{7,2},{8,13},{9,12},{10,... | collective-permute-start | bytes 32 | tf_op jit(solution)/shard_map/ppermute | solution.py:396
  104.5 3.6 %collective-permute-start.26 = (f32[2]{0:T(128)S(1)}, f32[2]{0:T(128)S(1)}, u32[]{:S(2)}, u32[]{:S(2)}) collective-permute-start(f32[2]{0:T(128)S(1)} %add.27), channel_id=1, source_target_pairs={{0,4},{1,5},{2,6},{3,7},{4,0},{5,1},{6,2},{7,3},{8,12},{9,13},{10,... | collective-permute-start | bytes 32 | tf_op jit(solution)/shard_map/ppermute | solution.py:396
  104.8 3.6 %collective-permute-start.25 = (f32[2]{0:T(128)S(1)}, f32[2]{0:T(128)S(1)}, u32[]{:S(2)}, u32[]{:S(2)}) collective-permute-start(f32[2]{0:T(128)S(1)} %add.27), channel_id=1, source_target_pairs={{0,1},{1,0},{2,3},{3,2},{4,5},{5,4},{6,7},{7,6},{8,9},{9,8},{10,11... | collective-permute-start | bytes 32 | tf_op jit(solution)/shard_map/ppermute | solution.py:396
  (4 other events, 16.2 us)

commit v2 on v1

--- a/solution.py
+++ b/solution.py
@@ -369,18 +369,24 @@
 
 
 def job_order(turns, stages):
-    jobs, far = [], []
-    singles = turns[:2] if len(turns) > 2 else turns[:1]
-    jobs += [(n, 0, True) for n in singles] + [(n, 1, None) for n in singles]
-    far += list(singles)
-    for n in turns[len(singles) :]:
-        jobs += [(n, 0, True), (far.pop(0), 0, False), (n, 1, None)]
-        far.append(n)
-    if stages == 3 and len(turns) > 2:
-        jobs += [(n, 2, None) for n in singles] + [(n, 0, False) for n in far]
-        return jobs + [(n, 2, None) for n in turns[len(singles) :]]
-    jobs += [(n, 0, False) for n in far]
-    return jobs + [(n, t, None) for t in range(2, stages) for n in turns]
+    def near(n):
+        return (n, 0, True)
+
+    def far(n):
+        return (n, 0, False)
+
+    def later(n, t=1):
+        return (n, t, None)
+
+    if stages == 3 and len(turns) == 4:
+        a, b, c, d = turns
+        jobs = [near(a), near(b), later(a), later(b), near(c), far(a), later(c), far(b), near(d)]
+        return jobs + [later(a, 2), later(b, 2), later(d), far(c), far(d), later(c, 2), later(d, 2)]
+    jobs = [near(turns[0])]
+    for n in turns:
+        jobs += [near(n + 1)] if n + 1 in turns else []
+        jobs.append(later(n))
+    return jobs + [far(n) for n in turns] + [later(n, t) for t in range(2, stages) for n in turns]
 
 
 def body(order, *arrays):

time: 109 us -> 105 us (0.963)
  starting transfers between devices: 23.6 us -> 20.3 us
  waiting for transfers between devices: 28.7 us -> 27.4 us
    ppermute x28, starting transfers between devices: 23.6 us -> 20.3 us  [swap(): return lax.ppermute(packet, GROUP, [(d, d ^ mask) for d in range(devices)])]
    ppermute x28, waiting for transfers between devices: 28.7 us -> 27.4 us  [swap(): return lax.ppermute(packet, GROUP, [(d, d ^ mask) for d in range(devices)])]
  transfers between devices with their start and end apart: 28 -> 28, of which waited for: 12 -> 12; matrix products, arithmetic and copies ran while one was open for 0% -> 0% of each run, Pallas kernels for 34% -> 40%
where the time goes in v2:
time: 105 us; the launch traced here: 104 us
  Pallas kernels  54.6 us (52%)
  waiting for transfers between devices  27.4 us (26%)
  starting transfers between devices  20.3 us (19%)
    pallas_call x16, Pallas kernels, send_call(): pl.pallas_call(functools.partial(send_kernel, cfg), in_specs=in_specs, ou...  43.4 us
    ppermute x28, waiting for transfers between devices, swap(): return lax.ppermute(packet, GROUP, [(d, d ^ mask) for d in range(devices)])  27.4 us
    ppermute x28, starting transfers between devices, swap(): return lax.ppermute(packet, GROUP, [(d, d ^ mask) for d in range(devices)])  20.3 us
    pallas_call x5, Pallas kernels, finish_call(): pl.pallas_call(functools.partial(finish_kernel, cfg), grid=(block_count,)...  9.22 us
  transfers between devices with their start and end apart: 28, of which 12 were waited for; matrix products, arithmetic and copies ran while one was open for 0% of the time, Pallas kernels for 40%

profile of v2, /device:TPU:0, one launch (start us, length us, event | category | flops | bytes accessed | tf_op | source)
XLA Modules:
  0.0 104.4 jit_solution(17734187300902471382)
XLA Ops:
  0.7 2.1 %open.1.refs_4_ = bf16[2,2,1536,256]{3,2,1,0:T(8,128)(2,1)S(1)} custom-call(bf16[2,1536,12288]{2,1,0:T(8,128)(2,1)} %refs_1_.31), custom_call_target="tpu_custom_call" | custom-call | tf_op jit(solution)/shard_map/open/pallas_call | solution.py:143
  3.2 2.5 %shard_map.86 = (s32[1288,128]{1,0:T(8,128)S(1)}, bf16[2,320,1536]{2,1,0:T(8,128)(2,1)S(1)}, bf16[2,2,1536,256]{3,2,1,0:T(8,128)(2,1)S(1)}) custom-call(bf16[2,320,1536]{2,1,0:T(8,128)(2,1)S(1)} %copy-done.1, bf16[2,1536,12288]{2,1,0:T(8,128)(2,1)} %refs_1_.31, s32[8]{0:T(128)S(1)} %copy-done.3, s32[8]{0:T(128)S(1)} %copy-done.5, ...), custom_call_target="tpu_custom_call" | custom-call | flops 1006632960 | bytes 3145728 | tf_op jit(solution)/shard_map/pallas_call | solution.py:265
  6.2 1.9 %shard_map.87 = (s32[1288,128]{1,0:T(8,128)S(1)}, bf16[2,2,1536,256]{3,2,1,0:T(8,128)(2,1)S(1)}) custom-call(bf16[2,320,1536]{2,1,0:T(8,128)(2,1)S(1)} %get-tuple-element.55.refs_0_.refs_1_, bf16[2,1536,12288]{2,1,0:T(8,128)(2,1)} %refs_1_.31, bf16[2,2,1536,256]{3,2,1,0:T(8,128)(2,1)S(1)} %get-tuple-element.56.refs_2_), custom_call_target="tpu_custom_call" | custom-call | flops 1006632960 | bytes 3145728 | tf_op jit(solution)/shard_map/pallas_call | solution.py:265
  8.2 1.9 %shard_map.88 = (s32[1288,128]{1,0:T(8,128)S(1)}, bf16[2,2,1536,256]{3,2,1,0:T(8,128)(2,1)S(1)}) custom-call(bf16[2,320,1536]{2,1,0:T(8,128)(2,1)S(1)} %get-tuple-element.55.refs_0_.refs_1_, bf16[2,1536,12288]{2,1,0:T(8,128)(2,1)} %refs_1_.31, bf16[2,2,1536,256]{3,2,1,0:T(8,128)(2,1)S(1)} %get-tuple-element.57.refs_2_, ...), custom_call_target="tpu_custom_call" | custom-call | flops 1006632960 | bytes 3145728 | tf_op jit(solution)/shard_map/pallas_call | solution.py:265
  10.3 2.9 %shard_map.89 = (s32[1288,128]{1,0:T(8,128)S(1)}, bf16[2,4,1536,256]{3,2,1,0:T(8,128)(2,1)S(1)}) custom-call(bf16[2,320,1536]{2,1,0:T(8,128)(2,1)S(1)} %get-tuple-element.55.refs_0_.refs_1_, bf16[2,1536,12288]{2,1,0:T(8,128)(2,1)} %refs_1_.31, bf16[2,2,1536,256]{3,2,1,0:T(8,128)(2,1)S(1)} %get-tuple-element.59.refs_2_, ...), custom_call_target="tpu_custom_call" | custom-call | flops 1006632960 | bytes 3145728 | tf_op jit(solution)/shard_map/pallas_call | solution.py:265
  13.3 2.7 %shard_map.90 = (s32[1288,128]{1,0:T(8,128)S(1)}, s32[1288,128]{1,0:T(8,128)S(1)}, bf16[2,2,1536,256]{3,2,1,0:T(8,128)(2,1)S(1)}) custom-call(bf16[2,320,1536]{2,1,0:T(8,128)(2,1)S(1)} %get-tuple-element.55.refs_0_.refs_1_, bf16[2,1536,12288]{2,1,0:T(8,128)(2,1)} %refs_1_.31, bf16[2,4,1536,256]{3,2,1,0:T(8,128)(2,1)S(1)} %get-tuple-element.61.refs_2_), custom_call_target="tpu_custom_call" | custom-call | flops 2013265920 | bytes 6291456 | tf_op jit(solution)/shard_map/pallas_call | solution.py:265
  16.5 2.8 %collective-permute-start.4 = (s32[1288,128]{1,0:T(8,128)S(1)}, s32[1288,128]{1,0:T(8,128)S(1)}, u32[]{:S(2)}, u32[]{:S(2)}) collective-permute-start(s32[1288,128]{1,0:T(8,128)S(1)} %get-tuple-element.69), channel_id=1, source_target_pairs={{0,1},{1,0},{2,3},{3,2},{4,5},{5,4},{6,7},{7,6},{8,9},{9,8},{10,11... | collective-permute-start | bytes 1978376 | tf_op jit(solution)/shard_map/ppermute | solution.py:402
  19.4 2.9 %shard_map.91 = (s32[1288,128]{1,0:T(8,128)S(1)}, bf16[2,4,1536,256]{3,2,1,0:T(8,128)(2,1)S(1)}) custom-call(bf16[2,320,1536]{2,1,0:T(8,128)(2,1)S(1)} %get-tuple-element.55.refs_0_.refs_1_, bf16[2,1536,12288]{2,1,0:T(8,128)(2,1)} %refs_1_.31, bf16[2,2,1536,256]{3,2,1,0:T(8,128)(2,1)S(1)} %get-tuple-element.62.refs_2_), custom_call_target="tpu_custom_call" | custom-call | flops 1006632960 | bytes 3145728 | tf_op jit(solution)/shard_map/pallas_call | solution.py:265
  22.4 1.6 %collective-permute-start.6 = (s32[1288,128]{1,0:T(8,128)S(1)}, s32[1288,128]{1,0:T(8,128)S(1)}, u32[]{:S(2)}, u32[]{:S(2)}) collective-permute-start(s32[1288,128]{1,0:T(8,128)S(1)} %get-tuple-element.72), channel_id=1, source_target_pairs={{0,4},{1,5},{2,6},{3,7},{4,0},{5,1},{6,2},{7,3},{8,12},{9,13},{10,... | collective-permute-start | bytes 1978376 | tf_op jit(solution)/shard_map/ppermute | solution.py:402
  24.0 2.8 %shard_map.92 = (s32[1288,128]{1,0:T(8,128)S(1)}, s32[1288,128]{1,0:T(8,128)S(1)}, bf16[2,2,1536,256]{3,2,1,0:T(8,128)(2,1)S(1)}) custom-call(bf16[2,320,1536]{2,1,0:T(8,128)(2,1)S(1)} %get-tuple-element.55.refs_0_.refs_1_, bf16[2,1536,12288]{2,1,0:T(8,128)(2,1)} %refs_1_.31, bf16[2,4,1536,256]{3,2,1,0:T(8,128)(2,1)S(1)} %get-tuple-element.63.refs_2_, ...), custom_call_target="tpu_custom_call" | custom-call | flops 2013265920 | bytes 6291456 | tf_op jit(solution)/shard_map/pallas_call | solution.py:265
  26.8 3.0 %shard_map.93 = (s32[1288,128]{1,0:T(8,128)S(1)}, bf16[2,4,1536,256]{3,2,1,0:T(8,128)(2,1)S(1)}) custom-call(bf16[2,320,1536]{2,1,0:T(8,128)(2,1)S(1)} %get-tuple-element.55.refs_0_.refs_1_, bf16[2,1536,12288]{2,1,0:T(8,128)(2,1)} %refs_1_.31, bf16[2,2,1536,256]{3,2,1,0:T(8,128)(2,1)S(1)} %get-tuple-element.66.refs_2_), custom_call_target="tpu_custom_call" | custom-call | flops 1006632960 | bytes 3145728 | tf_op jit(solution)/shard_map/pallas_call | solution.py:265
  30.0 2.7 %shard_map.94 = (s32[1288,128]{1,0:T(8,128)S(1)}, s32[1288,128]{1,0:T(8,128)S(1)}, bf16[2,2,1536,256]{3,2,1,0:T(8,128)(2,1)S(1)}) custom-call(bf16[2,320,1536]{2,1,0:T(8,128)(2,1)S(1)} %get-tuple-element.55.refs_0_.refs_1_, bf16[2,1536,12288]{2,1,0:T(8,128)(2,1)} %refs_1_.31, bf16[2,4,1536,256]{3,2,1,0:T(8,128)(2,1)S(1)} %get-tuple-element.67.refs_2_), custom_call_target="tpu_custom_call" | custom-call | flops 2013265920 | bytes 6291456 | tf_op jit(solution)/shard_map/pallas_call | solution.py:265
  34.5 1.7 %collective-permute-start.10 = (s32[1288,128]{1,0:T(8,128)S(1)}, s32[1288,128]{1,0:T(8,128)S(1)}, u32[]{:S(2)}, u32[]{:S(2)}) collective-permute-start(s32[1288,128]{1,0:T(8,128)S(1)} %get-tuple-element.80), channel_id=1, source_target_pairs={{0,1},{1,0},{2,3},{3,2},{4,5},{5,4},{6,7},{7,6},{8,9},{9,8},{10,11... | collective-permute-start | bytes 1978376 | tf_op jit(solution)/shard_map/ppermute | solution.py:402
  36.3 1.9 %shard_map.95 = (s32[648,128]{1,0:T(8,128)S(1)}, f32[2,320,256]{2,1,0:T(8,128)S(1)}, bf16[2,2,1536,256]{3,2,1,0:T(8,128)(2,1)S(1)}) custom-call(bf16[2,320,1536]{2,1,0:T(8,128)(2,1)S(1)} %get-tuple-element.55.refs_0_.refs_1_, bf16[2,1536,12288]{2,1,0:T(8,128)(2,1)} %refs_1_.31, bf16[2,2,1536,256]{3,2,1,0:T(8,128)(2,1)S(1)} %get-tuple-element.68.refs_2_, ...), custom_call_target="tpu_custom_call" | custom-call | flops 1006632960 | bytes 3145728 | tf_op jit(solution)/shard_map/pallas_call | solution.py:265
  39.6 1.5 %collective-permute-start.12 = (s32[1288,128]{1,0:T(8,128)S(1)}, s32[1288,128]{1,0:T(8,128)S(1)}, u32[]{:S(2)}, u32[]{:S(2)}) collective-permute-start(s32[1288,128]{1,0:T(8,128)S(1)} %get-tuple-element.82), channel_id=1, source_target_pairs={{0,4},{1,5},{2,6},{3,7},{4,0},{5,1},{6,2},{7,3},{8,12},{9,13},{10,... | collective-permute-start | bytes 1978376 | tf_op jit(solution)/shard_map/ppermute | solution.py:402
  41.1 2.9 %shard_map.96 = (s32[648,128]{1,0:T(8,128)S(1)}, f32[2,320,256]{2,1,0:T(8,128)S(1)}, bf16[2,4,1536,256]{3,2,1,0:T(8,128)(2,1)S(1)}) custom-call(bf16[2,320,1536]{2,1,0:T(8,128)(2,1)S(1)} %get-tuple-element.55.refs_0_.refs_1_, bf16[2,1536,12288]{2,1,0:T(8,128)(2,1)} %refs_1_.31, bf16[2,2,1536,256]{3,2,1,0:T(8,128)(2,1)S(1)} %get-tuple-element.71.refs_2_, ...), custom_call_target="tpu_custom_call" | custom-call | flops 1006632960 | bytes 3145728 | tf_op jit(solution)/shard_map/pallas_call | solution.py:265
  44.1 3.0 %shard_map.97 = (s32[1288,128]{1,0:T(8,128)S(1)}, s32[1288,128]{1,0:T(8,128)S(1)}, bf16[2,4,1536,256]{3,2,1,0:T(8,128)(2,1)S(1)}) custom-call(bf16[2,320,1536]{2,1,0:T(8,128)(2,1)S(1)} %get-tuple-element.55.refs_0_.refs_1_, bf16[2,1536,12288]{2,1,0:T(8,128)(2,1)} %refs_1_.31, bf16[2,4,1536,256]{3,2,1,0:T(8,128)(2,1)S(1)} %get-tuple-element.74.refs_2_, ...), custom_call_target="tpu_custom_call" | custom-call | flops 2013265920 | bytes 6291456 | tf_op jit(solution)/shard_map/pallas_call | solution.py:265
  47.1 3.0 %shard_map.98 = (s32[1288,128]{1,0:T(8,128)S(1)}, s32[1288,128]{1,0:T(8,128)S(1)}, bf16[2,4,1536,256]{3,2,1,0:T(8,128)(2,1)S(1)}) custom-call(bf16[2,320,1536]{2,1,0:T(8,128)(2,1)S(1)} %get-tuple-element.55.refs_0_.refs_1_, bf16[2,1536,12288]{2,1,0:T(8,128)(2,1)} %refs_1_.31, bf16[2,4,1536,256]{3,2,1,0:T(8,128)(2,1)S(1)} %get-tuple-element.77.refs_2_), custom_call_target="tpu_custom_call" | custom-call | flops 2013265920 | bytes 6291456 | tf_op jit(solution)/shard_map/pallas_call | solution.py:265
  51.2 2.9 %shard_map.99 = (s32[1288,128]{1,0:T(8,128)S(1)}, s32[1288,128]{1,0:T(8,128)S(1)}, bf16[2,4,1536,256]{3,2,1,0:T(8,128)(2,1)S(1)}) custom-call(bf16[2,320,1536]{2,1,0:T(8,128)(2,1)S(1)} %get-tuple-element.55.refs_0_.refs_1_, bf16[2,1536,12288]{2,1,0:T(8,128)(2,1)} %refs_1_.31, bf16[2,4,1536,256]{3,2,1,0:T(8,128)(2,1)S(1)} %get-tuple-element.78.refs_2_), custom_call_target="tpu_custom_call" | custom-call | flops 2013265920 | bytes 6291456 | tf_op jit(solution)/shard_map/pallas_call | solution.py:265
  54.2 1.7 %collective-permute-done.12.refs_5_.refs_10_ = s32[1288,128]{1,0:T(8,128)S(1)} collective-permute-done((s32[1288,128]{1,0:T(8,128)S(1)}, s32[1288,128]{1,0:T(8,128)S(1)}, u32[]{:S(2)}, u32[]{:S(2)}) %collective-permute-start.12) | collective-permute-done | bytes 659488 | tf_op jit(solution)/shard_map/ppermute | solution.py:402
  55.9 1.5 %collective-permute-start.16 = (s32[1288,128]{1,0:T(8,128)S(1)}, s32[1288,128]{1,0:T(8,128)S(1)}, u32[]{:S(2)}, u32[]{:S(2)}) collective-permute-start(s32[1288,128]{1,0:T(8,128)S(1)} %get-tuple-element.87), channel_id=1, source_target_pairs={{0,4},{1,5},{2,6},{3,7},{4,0},{5,1},{6,2},{7,3},{8,12},{9,13},{10,... | collective-permute-start | bytes 1978376 | tf_op jit(solution)/shard_map/ppermute | solution.py:402
  58.0 3.2 %shard_map.100 = (s32[648,128]{1,0:T(8,128)S(1)}, s32[648,128]{1,0:T(8,128)S(1)}, f32[2,320,512]{2,1,0:T(8,128)S(1)}, bf16[2,4,1536,256]{3,2,1,0:T(8,128)(2,1)S(1)}) custom-call(bf16[2,320,1536]{2,1,0:T(8,128)(2,1)S(1)} %get-tuple-element.55.refs_0_.refs_1_, bf16[2,1536,12288]{2,1,0:T(8,128)(2,1)} %refs_1_.31, ...), custom_call_target="tpu_custom_call" | custom-call | flops 2013265920 | bytes 6291456 | tf_op jit(solution)/shard_map/pallas_call | solution.py:265
  61.2 6.2 %collective-permute-done.14.refs_3_.refs_8_ = s32[1288,128]{1,0:T(8,128)S(1)} collective-permute-done((s32[1288,128]{1,0:T(8,128)S(1)}, s32[1288,128]{1,0:T(8,128)S(1)}, u32[]{:S(2)}, u32[]{:S(2)}) %collective-permute-start.14) | collective-permute-done | bytes 659488 | tf_op jit(solution)/shard_map/ppermute | solution.py:402
  68.0 5.6 %collective-permute-done.16.refs_5_.refs_10_ = s32[1288,128]{1,0:T(8,128)S(1)} collective-permute-done((s32[1288,128]{1,0:T(8,128)S(1)}, s32[1288,128]{1,0:T(8,128)S(1)}, u32[]{:S(2)}, u32[]{:S(2)}) %collective-permute-start.16) | collective-permute-done | bytes 659488 | tf_op jit(solution)/shard_map/ppermute | solution.py:402
  73.6 3.1 %shard_map.101 = (s32[648,128]{1,0:T(8,128)S(1)}, s32[648,128]{1,0:T(8,128)S(1)}, f32[2,320,512]{2,1,0:T(8,128)S(1)}) custom-call(bf16[2,320,1536]{2,1,0:T(8,128)(2,1)S(1)} %get-tuple-element.55.refs_0_.refs_1_, bf16[2,1536,12288]{2,1,0:T(8,128)(2,1)} %refs_1_.31, bf16[2,4,1536,256]{3,2,1,0:T(8,128)(2,1)S(1)} %get-tuple-element.84.refs_2_, ...), custom_call_target="tpu_custom_call" | custom-call | flops 2013265920 | bytes 6291456 | tf_op jit(solution)/shard_map/pallas_call | solution.py:265
  76.8 1.6 %collective-permute-start.19 = (s32[648,128]{1,0:T(8,128)S(1)}, s32[648,128]{1,0:T(8,128)S(1)}, u32[]{:S(2)}, u32[]{:S(2)}) collective-permute-start(s32[648,128]{1,0:T(8,128)S(1)} %get-tuple-element.93), channel_id=1, source_target_pairs={{0,4},{1,5},{2,6},{3,7},{4,0},{5,1},{6,2},{7,3},{8,12},{9,13},{10,... | collective-permute-start | bytes 995336 | tf_op jit(solution)/shard_map/ppermute | solution.py:402
  81.3 1.8 %shard_map.102 = (bf16[2,320,1536]{2,1,0:T(8,128)(2,1)}, f32[2,8,128]{2,1,0:T(8,128)S(1)}, f32[2,320,128]{2,1,0:T(8,128)S(1)}) custom-call(f32[2,320,256]{2,1,0:T(8,128)S(1)} %get-tuple-element.90.refs_0_, bf16[2,320,1536]{2,1,0:T(8,128)(2,1)S(1)} %get-tuple-element.55.refs_0_.refs_1_, f32[2,320]{1,0:T(2,128)S(1)} %copy-done.7, f32[2,1536]{1,0:T(2,128)S(1)} %copy-done.2, ...), custom_call_target="tpu_custom_call" | custom-call | flops 9830400 | bytes 1638400 | tf_op jit(solution)/shard_map/pallas_call | solution.py:357
  83.1 1.7 %shard_map.103 = (bf16[2,320,1536]{2,1,0:T(8,128)(2,1)}, f32[2,8,128]{2,1,0:T(8,128)S(1)}) custom-call(f32[2,320,256]{2,1,0:T(8,128)S(1)} %get-tuple-element.100.refs_0_, bf16[2,320,1536]{2,1,0:T(8,128)(2,1)S(1)} %get-tuple-element.55.refs_0_.refs_1_, f32[2,320,128]{2,1,0:T(8,128)S(1)} %get-tuple-element.92.refs_2_, ...), custom_call_target="tpu_custom_call", output_to_operand_aliasing={{0}: (7, {})} | custom-call | flops 9830400 | bytes 1638400 | tf_op jit(solution)/shard_map/pallas_call | solution.py:357
  84.8 3.0 %collective-permute-done.19.refs_6_ = s32[648,128]{1,0:T(8,128)S(1)} collective-permute-done((s32[648,128]{1,0:T(8,128)S(1)}, s32[648,128]{1,0:T(8,128)S(1)}, u32[]{:S(2)}, u32[]{:S(2)}) %collective-permute-start.19) | collective-permute-done | bytes 331808 | tf_op jit(solution)/shard_map/ppermute | solution.py:402
  89.2 3.6 %collective-permute-done.21.refs_6_ = s32[648,128]{1,0:T(8,128)S(1)} collective-permute-done((s32[648,128]{1,0:T(8,128)S(1)}, s32[648,128]{1,0:T(8,128)S(1)}, u32[]{:S(2)}, u32[]{:S(2)}) %collective-permute-start.21) | collective-permute-done | bytes 331808 | tf_op jit(solution)/shard_map/ppermute | solution.py:402
  92.8 2.2 %shard_map.104 = (bf16[2,320,1536]{2,1,0:T(8,128)(2,1)}, f32[2,8,128]{2,1,0:T(8,128)S(1)}) custom-call(f32[2,320,512]{2,1,0:T(8,128)S(1)} %get-tuple-element.95.refs_0_, bf16[2,320,1536]{2,1,0:T(8,128)(2,1)S(1)} %get-tuple-element.55.refs_0_.refs_1_, f32[2,320,128]{2,1,0:T(8,128)S(1)} %get-tuple-element.92.refs_2_, ...), custom_call_target="tpu_custom_call", output_to_operand_aliasing={{0}: (8, {})} | custom-call | flops 19660800 | bytes 3276800 | tf_op jit(solution)/shard_map/pallas_call | solution.py:357
  95.1 2.2 %shard_map.105 = bf16[2,320,1536]{2,1,0:T(8,128)(2,1)} custom-call(f32[2,320,512]{2,1,0:T(8,128)S(1)} %get-tuple-element.89.refs_0_, bf16[2,320,1536]{2,1,0:T(8,128)(2,1)S(1)} %get-tuple-element.55.refs_0_.refs_1_, f32[2,320,128]{2,1,0:T(8,128)S(1)} %get-tuple-element.92.refs_2_, f32[2,1536]{1,0:T(2,128)S(1)} %copy-done.2, ...), custom_call_target="tpu_custom_call", output_to_operand_aliasing={{}: (8, {})} | custom-call | flops 19660800 | bytes 3276800 | tf_op jit(solution)/shard_map/pallas_call | solution.py:357
  (65 shorter events, 19.3 us)
Async XLA Ops:
  5.7 2.6 %collective-permute-start = (s32[1288,128]{1,0:T(8,128)S(1)}, s32[1288,128]{1,0:T(8,128)S(1)}, u32[]{:S(2)}, u32[]{:S(2)}) collective-permute-start(s32[1288,128]{1,0:T(8,128)S(1)} %get-tuple-element.58), channel_id=1, source_target_pairs={{0,2},{1,3},{2,0},{3,1},{4,6},{5,7},{6,4},{7,5},{8,10},{9,11},{10,... | collective-permute-start | bytes 1978376 | tf_op jit(solution)/shard_map/ppermute | solution.py:402
  8.1 2.2 %collective-permute-start.1 = (s32[1288,128]{1,0:T(8,128)S(1)}, s32[1288,128]{1,0:T(8,128)S(1)}, u32[]{:S(2)}, u32[]{:S(2)}) collective-permute-start(s32[1288,128]{1,0:T(8,128)S(1)} %get-tuple-element.60), channel_id=1, source_target_pairs={{0,2},{1,3},{2,0},{3,1},{4,6},{5,7},{6,4},{7,5},{8,10},{9,11},{10,... | collective-permute-start | bytes 1978376 | tf_op jit(solution)/shard_map/ppermute | solution.py:402
  16.0 8.0 %collective-permute-start.2 = (s32[1288,128]{1,0:T(8,128)S(1)}, s32[1288,128]{1,0:T(8,128)S(1)}, u32[]{:S(2)}, u32[]{:S(2)}) collective-permute-start(s32[1288,128]{1,0:T(8,128)S(1)} %get-tuple-element.64), channel_id=1, source_target_pairs={{0,2},{1,3},{2,0},{3,1},{4,6},{5,7},{6,4},{7,5},{8,10},{9,11},{10,... | collective-permute-start | bytes 1978376 | tf_op jit(solution)/shard_map/ppermute | solution.py:402
  16.4 7.6 %collective-permute-start.3 = (s32[1288,128]{1,0:T(8,128)S(1)}, s32[1288,128]{1,0:T(8,128)S(1)}, u32[]{:S(2)}, u32[]{:S(2)}) collective-permute-start(s32[1288,128]{1,0:T(8,128)S(1)} %get-tuple-element.65), channel_id=1, source_target_pairs={{0,2},{1,3},{2,0},{3,1},{4,6},{5,7},{6,4},{7,5},{8,10},{9,11},{10,... | collective-permute-start | bytes 1978376 | tf_op jit(solution)/shard_map/ppermute | solution.py:402
  16.5 18.0 %collective-permute-start.4 = (s32[1288,128]{1,0:T(8,128)S(1)}, s32[1288,128]{1,0:T(8,128)S(1)}, u32[]{:S(2)}, u32[]{:S(2)}) collective-permute-start(s32[1288,128]{1,0:T(8,128)S(1)} %get-tuple-element.69), channel_id=1, source_target_pairs={{0,1},{1,0},{2,3},{3,2},{4,5},{5,4},{6,7},{7,6},{8,9},{9,8},{10,11... | collective-permute-start | bytes 1978376 | tf_op jit(solution)/shard_map/ppermute | solution.py:402
  22.3 12.2 %collective-permute-start.5 = (s32[1288,128]{1,0:T(8,128)S(1)}, s32[1288,128]{1,0:T(8,128)S(1)}, u32[]{:S(2)}, u32[]{:S(2)}) collective-permute-start(s32[1288,128]{1,0:T(8,128)S(1)} %get-tuple-element.70), channel_id=1, source_target_pairs={{0,2},{1,3},{2,0},{3,1},{4,6},{5,7},{6,4},{7,5},{8,10},{9,11},{10,... | collective-permute-start | bytes 1978376 | tf_op jit(solution)/shard_map/ppermute | solution.py:402
  22.4 17.2 %collective-permute-start.6 = (s32[1288,128]{1,0:T(8,128)S(1)}, s32[1288,128]{1,0:T(8,128)S(1)}, u32[]{:S(2)}, u32[]{:S(2)}) collective-permute-start(s32[1288,128]{1,0:T(8,128)S(1)} %get-tuple-element.72), channel_id=1, source_target_pairs={{0,4},{1,5},{2,6},{3,7},{4,0},{5,1},{6,2},{7,3},{8,12},{9,13},{10,... | collective-permute-start | bytes 1978376 | tf_op jit(solution)/shard_map/ppermute | solution.py:402
  29.7 11.4 %collective-permute-start.7 = (s32[1288,128]{1,0:T(8,128)S(1)}, s32[1288,128]{1,0:T(8,128)S(1)}, u32[]{:S(2)}, u32[]{:S(2)}) collective-permute-start(s32[1288,128]{1,0:T(8,128)S(1)} %get-tuple-element.73), channel_id=1, source_target_pairs={{0,2},{1,3},{2,0},{3,1},{4,6},{5,7},{6,4},{7,5},{8,10},{9,11},{10,... | collective-permute-start | bytes 1978376 | tf_op jit(solution)/shard_map/ppermute | solution.py:402
  32.7 11.4 %collective-permute-start.8 = (s32[1288,128]{1,0:T(8,128)S(1)}, s32[1288,128]{1,0:T(8,128)S(1)}, u32[]{:S(2)}, u32[]{:S(2)}) collective-permute-start(s32[1288,128]{1,0:T(8,128)S(1)} %get-tuple-element.75), channel_id=1, source_target_pairs={{0,2},{1,3},{2,0},{3,1},{4,6},{5,7},{6,4},{7,5},{8,10},{9,11},{10,... | collective-permute-start | bytes 1978376 | tf_op jit(solution)/shard_map/ppermute | solution.py:402
  34.5 9.6 %collective-permute-start.9 = (s32[1288,128]{1,0:T(8,128)S(1)}, s32[1288,128]{1,0:T(8,128)S(1)}, u32[]{:S(2)}, u32[]{:S(2)}) collective-permute-start(s32[1288,128]{1,0:T(8,128)S(1)} %get-tuple-element.76), channel_id=1, source_target_pairs={{0,2},{1,3},{2,0},{3,1},{4,6},{5,7},{6,4},{7,5},{8,10},{9,11},{10,... | collective-permute-start | bytes 1978376 | tf_op jit(solution)/shard_map/ppermute | solution.py:402
  34.5 19.6 %collective-permute-start.10 = (s32[1288,128]{1,0:T(8,128)S(1)}, s32[1288,128]{1,0:T(8,128)S(1)}, u32[]{:S(2)}, u32[]{:S(2)}) collective-permute-start(s32[1288,128]{1,0:T(8,128)S(1)} %get-tuple-element.80), channel_id=1, source_target_pairs={{0,1},{1,0},{2,3},{3,2},{4,5},{5,4},{6,7},{7,6},{8,9},{9,8},{10,11... | collective-permute-start | bytes 1978376 | tf_op jit(solution)/shard_map/ppermute | solution.py:402
  39.6 16.3 %collective-permute-start.12 = (s32[1288,128]{1,0:T(8,128)S(1)}, s32[1288,128]{1,0:T(8,128)S(1)}, u32[]{:S(2)}, u32[]{:S(2)}) collective-permute-start(s32[1288,128]{1,0:T(8,128)S(1)} %get-tuple-element.82), channel_id=1, source_target_pairs={{0,4},{1,5},{2,6},{3,7},{4,0},{5,1},{6,2},{7,3},{8,12},{9,13},{10,... | collective-permute-start | bytes 1978376 | tf_op jit(solution)/shard_map/ppermute | solution.py:402
  50.0 7.4 %collective-permute-start.11 = (s32[1288,128]{1,0:T(8,128)S(1)}, s32[1288,128]{1,0:T(8,128)S(1)}, u32[]{:S(2)}, u32[]{:S(2)}) collective-permute-start(s32[1288,128]{1,0:T(8,128)S(1)} %get-tuple-element.81), channel_id=1, source_target_pairs={{0,2},{1,3},{2,0},{3,1},{4,6},{5,7},{6,4},{7,5},{8,10},{9,11},{10,... | collective-permute-start | bytes 1978376 | tf_op jit(solution)/shard_map/ppermute | solution.py:402
  50.1 7.3 %collective-permute-start.13 = (s32[1288,128]{1,0:T(8,128)S(1)}, s32[1288,128]{1,0:T(8,128)S(1)}, u32[]{:S(2)}, u32[]{:S(2)}) collective-permute-start(s32[1288,128]{1,0:T(8,128)S(1)} %get-tuple-element.83), channel_id=1, source_target_pairs={{0,2},{1,3},{2,0},{3,1},{4,6},{5,7},{6,4},{7,5},{8,10},{9,11},{10,... | collective-permute-start | bytes 1978376 | tf_op jit(solution)/shard_map/ppermute | solution.py:402
  50.6 16.8 %collective-permute-start.14 = (s32[1288,128]{1,0:T(8,128)S(1)}, s32[1288,128]{1,0:T(8,128)S(1)}, u32[]{:S(2)}, u32[]{:S(2)}) collective-permute-start(s32[1288,128]{1,0:T(8,128)S(1)} %get-tuple-element.85), channel_id=1, source_target_pairs={{0,1},{1,0},{2,3},{3,2},{4,5},{5,4},{6,7},{7,6},{8,9},{9,8},{10,11... | collective-permute-start | bytes 1978376 | tf_op jit(solution)/shard_map/ppermute | solution.py:402
  54.1 13.8 %collective-permute-start.15 = (s32[1288,128]{1,0:T(8,128)S(1)}, s32[1288,128]{1,0:T(8,128)S(1)}, u32[]{:S(2)}, u32[]{:S(2)}) collective-permute-start(s32[1288,128]{1,0:T(8,128)S(1)} %get-tuple-element.86), channel_id=1, source_target_pairs={{0,2},{1,3},{2,0},{3,1},{4,6},{5,7},{6,4},{7,5},{8,10},{9,11},{10,... | collective-permute-start | bytes 1978376 | tf_op jit(solution)/shard_map/ppermute | solution.py:402
  55.9 17.7 %collective-permute-start.16 = (s32[1288,128]{1,0:T(8,128)S(1)}, s32[1288,128]{1,0:T(8,128)S(1)}, u32[]{:S(2)}, u32[]{:S(2)}) collective-permute-start(s32[1288,128]{1,0:T(8,128)S(1)} %get-tuple-element.87), channel_id=1, source_target_pairs={{0,4},{1,5},{2,6},{3,7},{4,0},{5,1},{6,2},{7,3},{8,12},{9,13},{10,... | collective-permute-start | bytes 1978376 | tf_op jit(solution)/shard_map/ppermute | solution.py:402
  57.4 16.2 %collective-permute-start.17 = (s32[1288,128]{1,0:T(8,128)S(1)}, s32[1288,128]{1,0:T(8,128)S(1)}, u32[]{:S(2)}, u32[]{:S(2)}) collective-permute-start(s32[1288,128]{1,0:T(8,128)S(1)} %get-tuple-element.88), channel_id=1, source_target_pairs={{0,2},{1,3},{2,0},{3,1},{4,6},{5,7},{6,4},{7,5},{8,10},{9,11},{10,... | collective-permute-start | bytes 1978376 | tf_op jit(solution)/shard_map/ppermute | solution.py:402
  57.5 23.3 %collective-permute-start.18 = (s32[648,128]{1,0:T(8,128)S(1)}, s32[648,128]{1,0:T(8,128)S(1)}, u32[]{:S(2)}, u32[]{:S(2)}) collective-permute-start(s32[648,128]{1,0:T(8,128)S(1)} %get-tuple-element.91), channel_id=1, source_target_pairs={{0,4},{1,5},{2,6},{3,7},{4,0},{5,1},{6,2},{7,3},{8,12},{9,13},{10,... | collective-permute-start | bytes 995336 | tf_op jit(solution)/shard_map/ppermute | solution.py:402
  67.4 15.7 %collective-permute-start.23 = (s32[648,128]{1,0:T(8,128)S(1)}, s32[648,128]{1,0:T(8,128)S(1)}, u32[]{:S(2)}, u32[]{:S(2)}) collective-permute-start(s32[648,128]{1,0:T(8,128)S(1)} %get-tuple-element.101), channel_id=1, source_target_pairs={{0,1},{1,0},{2,3},{3,2},{4,5},{5,4},{6,7},{7,6},{8,9},{9,8},{10,11... | collective-permute-start | bytes 995336 | tf_op jit(solution)/shard_map/ppermute | solution.py:402
  73.6 7.7 %copy-start.2 = (f32[2,1536]{1,0:T(2,128)S(1)}, f32[2,1536]{1,0:T(2,128)}, u32[]{:S(2)}) copy-start(f32[2,1536]{1,0:T(2,128)} %refs_3_.11) | copy-start | bytes 36868
  73.6 7.7 %copy-start.4 = (s32[8]{0:T(128)S(1)}, s32[8]{0:T(128)}, u32[]{:S(2)}) copy-start(s32[8]{0:T(128)} %refs_4_.9) | copy-start | bytes 100
  73.6 7.7 %copy-start.6 = (s32[8]{0:T(128)S(1)}, s32[8]{0:T(128)}, u32[]{:S(2)}) copy-start(s32[8]{0:T(128)} %refs_5_.13) | copy-start | bytes 100
  73.6 7.7 %copy-start.7 = (f32[2,320]{1,0:T(2,128)S(1)}, f32[2,320]{1,0:T(2,128)}, u32[]{:S(2)}) copy-start(f32[2,320]{1,0:T(2,128)} %refs_2_.3) | copy-start | bytes 7684
  76.8 11.1 %collective-permute-start.19 = (s32[648,128]{1,0:T(8,128)S(1)}, s32[648,128]{1,0:T(8,128)S(1)}, u32[]{:S(2)}, u32[]{:S(2)}) collective-permute-start(s32[648,128]{1,0:T(8,128)S(1)} %get-tuple-element.93), channel_id=1, source_target_pairs={{0,4},{1,5},{2,6},{3,7},{4,0},{5,1},{6,2},{7,3},{8,12},{9,13},{10,... | collective-permute-start | bytes 995336 | tf_op jit(solution)/shard_map/ppermute | solution.py:402
  78.4 9.5 %collective-permute-start.20 = (s32[648,128]{1,0:T(8,128)S(1)}, s32[648,128]{1,0:T(8,128)S(1)}, u32[]{:S(2)}, u32[]{:S(2)}) collective-permute-start(s32[648,128]{1,0:T(8,128)S(1)} %get-tuple-element.94), channel_id=1, source_target_pairs={{0,1},{1,0},{2,3},{3,2},{4,5},{5,4},{6,7},{7,6},{8,9},{9,8},{10,11... | collective-permute-start | bytes 995336 | tf_op jit(solution)/shard_map/ppermute | solution.py:402
  78.9 13.9 %collective-permute-start.21 = (s32[648,128]{1,0:T(8,128)S(1)}, s32[648,128]{1,0:T(8,128)S(1)}, u32[]{:S(2)}, u32[]{:S(2)}) collective-permute-start(s32[648,128]{1,0:T(8,128)S(1)} %get-tuple-element.97), channel_id=1, source_target_pairs={{0,4},{1,5},{2,6},{3,7},{4,0},{5,1},{6,2},{7,3},{8,12},{9,13},{10,... | collective-permute-start | bytes 995336 | tf_op jit(solution)/shard_map/ppermute | solution.py:402
  80.7 12.1 %collective-permute-start.22 = (s32[648,128]{1,0:T(8,128)S(1)}, s32[648,128]{1,0:T(8,128)S(1)}, u32[]{:S(2)}, u32[]{:S(2)}) collective-permute-start(s32[648,128]{1,0:T(8,128)S(1)} %get-tuple-element.99), channel_id=1, source_target_pairs={{0,1},{1,0},{2,3},{3,2},{4,5},{5,4},{6,7},{7,6},{8,9},{9,8},{10,11... | collective-permute-start | bytes 995336 | tf_op jit(solution)/shard_map/ppermute | solution.py:402
  95.1 2.2 %collective-permute-start.24 = (f32[2]{0:T(128)S(1)}, f32[2]{0:T(128)S(1)}, u32[]{:S(2)}, u32[]{:S(2)}) collective-permute-start(f32[2]{0:T(128)S(1)} %add_reduce_fusion), channel_id=1, source_target_pairs={{0,2},{1,3},{2,0},{3,1},{4,6},{5,7},{6,4},{7,5},{8,10},{9,11},{10,... | collective-permute-start | bytes 32 | tf_op jit(solution)/shard_map/ppermute | solution.py:402
  97.3 4.5 %collective-permute-start.27 = (f32[2]{0:T(128)S(1)}, f32[2]{0:T(128)S(1)}, u32[]{:S(2)}, u32[]{:S(2)}) collective-permute-start(f32[2]{0:T(128)S(1)} %add.27), channel_id=1, source_target_pairs={{0,5},{1,4},{2,7},{3,6},{4,1},{5,0},{6,3},{7,2},{8,13},{9,12},{10,... | collective-permute-start | bytes 32 | tf_op jit(solution)/shard_map/ppermute | solution.py:402
  98.7 3.6 %collective-permute-start.26 = (f32[2]{0:T(128)S(1)}, f32[2]{0:T(128)S(1)}, u32[]{:S(2)}, u32[]{:S(2)}) collective-permute-start(f32[2]{0:T(128)S(1)} %add.27), channel_id=1, source_target_pairs={{0,4},{1,5},{2,6},{3,7},{4,0},{5,1},{6,2},{7,3},{8,12},{9,13},{10,... | collective-permute-start | bytes 32 | tf_op jit(solution)/shard_map/ppermute | solution.py:402
  100.3 3.6 %collective-permute-start.25 = (f32[2]{0:T(128)S(1)}, f32[2]{0:T(128)S(1)}, u32[]{:S(2)}, u32[]{:S(2)}) collective-permute-start(f32[2]{0:T(128)S(1)} %add.27), channel_id=1, source_target_pairs={{0,1},{1,0},{2,3},{3,2},{4,5},{5,4},{6,7},{7,6},{8,9},{9,8},{10,11... | collective-permute-start | bytes 32 | tf_op jit(solution)/shard_map/ppermute | solution.py:402
  (4 other events, 13.9 us)
